TPU v7x, 256 devices: a whole 4x4x8 slice. The times are simulated.
256 devices in a mesh: ang: 16 (over x, z_hi, core), tile: 16 (over y, z_lo).
Axes of the slice: x: 4, y: 4, z: 8 (z_hi: 2, z_lo: 4; z = z_hi * 4 + z_lo), core: 2. Of those that a mesh axis runs over, the one named last changes fastest.
Arguments:
- volume: float32 [256, 128, 256], P('ang', 'tile'), may hold values from -6 to 6
- phase: float32 [16, 128, 256], P('ang', 'tile'), may hold values from -6 to 6
- dual: float32 [16, 128, 256], P('ang', 'tile'), may hold values from -3 to 3
- probe_real: float32 [128, 128], replicated, may hold values from -4 to 4
- probe_imag: float32 [128, 128], replicated, may hold values from -4 to 4
- intensity: float32 [16, 64, 128, 128], P('ang', 'tile'), may hold values from 0.05 to 4
- offsets: int32 [16, 64], P('ang', 'tile'), may hold values from 0 to 128
- angle_index: int32 [16], P('ang'), may hold values from 0 to 180
Outputs:
- phase_new: float32 [16, 128, 256], P('ang', 'tile')
- volume_new: float32 [256, 128, 256], P('ang', 'tile')
- dual_new: float32 [16, 128, 256], P('ang', 'tile')
Inputs may be any that keep to these rules, and one draw needn't show every extreme that they name: `offsets`: the probe's 128 columns starting at the offset lie inside the 256 columns of a projection.
All inputs are finite; a program needn't handle non-finite values.
Results may differ from a plain program's by a relative error of at most 0.015.
Values may be sent and summed in bfloat16 or wider, within the bound.
A program may use at most 64 MiB of HBM per device.

v0:
```python
import math

import jax
import jax.numpy as jnp
import numpy as np
from jax import lax
from jax.experimental import pallas as pl
from jax.experimental.pallas import tpu as pltpu
from jax.sharding import PartitionSpec as P

angle_center = 90.0
rho_weight = 1.0
eta_step = 0.01
tau_step = 1.0
smooth_weight = 0.25

N = 256
HALF = 128
PEERS = 8
TILES = 16
ROWS = 16
SHOTS = 4
F32 = jnp.float32
BF16 = jnp.bfloat16
MESH = pl.DeviceIdType.MESH


def tables_of(length):
    index = np.arange(length)
    phases = (index[:, None] * index[None, :] % length).astype(np.float32)
    phases = phases * np.float32(2.0 * math.pi / length)
    return np.cos(phases), np.sin(phases)


def packed_tables():
    cos, sin = tables_of(N)
    signs = np.where(np.arange(N) % 2 == 0, 1.0, -1.0)
    forward = np.concatenate([cos[:, :HALF], -sin[:, :HALF]], axis=1)
    forward[:, HALF] = signs
    inverse = np.concatenate([2.0 * cos[:HALF], -2.0 * sin[:HALF]], axis=0)
    inverse[0] = 1.0
    inverse[HALF] = signs
    inverse = inverse / N
    cos, sin = tables_of(HALF)
    cos, sin = cos / math.sqrt(HALF), sin / math.sqrt(HALF)
    near = np.block([[cos, -sin], [sin, cos]])
    away = np.block([[cos, sin], [-sin, cos]])
    stack = np.stack([forward, inverse, forward.T, inverse.T, near, away])
    return stack.astype(np.float32)


def sincos_turns(turns):
    a = (turns - jnp.floor(turns + 0.5)) * math.pi
    z = a * a
    sin = 1.0
    for k in (12, 10, 8, 6, 4, 2):
        sin = 1.0 - z * sin * (1.0 / (k * (k + 1)))
    sin = a * sin
    cos = 1.0
    for k in (13, 11, 9, 7, 5, 3, 1):
        cos = 1.0 - z * cos * (1.0 / (k * (k + 1)))
    return 2.0 * sin * cos, 1.0 - 2.0 * sin * sin


def dot(a, b):
    return jnp.dot(a, b, preferred_element_type=F32)


def two_parts(x):
    high = x.astype(BF16)
    low = (x - high.astype(F32)).astype(BF16)
    return jnp.concatenate([high, low], axis=0)


def dot_parts(x, table):
    both = dot(two_parts(x), table)
    return both[: x.shape[0]] + both[x.shape[0] :]


def step_kernel(
    offsets_ref, angle_ref, vol_ref, phase_ref, dual_ref, pr_ref, pi_ref, inten_ref, tab_ref,
    phase_out, vol_out, dual_out,
    coef_send, coef_all, v_send, v_all, b_send, b_all, b_own, halo, phase_all, g_send, g_all, l_send, l_all,
    old_send, old_all, new_send, new_all, k_send, k_all, s_send, s_recv,
    tab_a, tab_b, xs, xb, s_sum, spec, wave,
    phase_ss, phase_rs, g_ss, g_rs, coef_ss, coef_rs, v_ss, v_rs, b_ss, b_rs, l_ss, l_rs,
    old_ss, old_rs, new_ss, new_rs, k_ss, k_rs, one_ss, one_rs,
):
    me = lax.axis_index("ang")
    tile = lax.axis_index("tile")
    core = me % 2
    mine = me // 2
    x_me, hi_me = mine // 2, mine % 2
    low = tile % 4
    far_tile = (tile // 4) * 4 + (low + 2) % 4
    turn_out = (low + 2) // 4
    turn_in = ((low + 2) % 4 + 2) // 4
    my_slot = 2 * x_me + (hi_me + turn_in) % 2
    twin = (me - core + (1 - core), tile)

    def peer(p):
        return (2 * p + core, far_tile)

    def slot_of(p):
        return 2 * (p // 2) + (p % 2 + turn_out) % 2

    def beside(o):
        return (me, (tile + o) % TILES)

    barrier = pltpu.get_barrier_semaphore()
    for o in range(1, TILES):
        pl.semaphore_signal(barrier, inc=1, device_id=beside(o), device_id_type=MESH)
    for p in range(PEERS):
        pl.semaphore_signal(barrier, inc=1, device_id=peer(p), device_id_type=MESH)
    pl.semaphore_signal(barrier, inc=1, device_id=twin, device_id_type=MESH)

    fwd_x, inv_x, fwd_y, inv_y, near, away = (tab_ref[i] for i in range(6))

    number = jnp.full((8, 128), angle_ref[0], jnp.int32).astype(F32) - angle_center
    sin_b, unused = sincos_turns(number * (1.0 / 720.0))
    sin_h, cos_h = sincos_turns(number * (1.0 / 1440.0))
    rows8 = lax.broadcasted_iota(jnp.int32, (8, 128), 0)
    coef_send[...] = jnp.where(rows8 < 4, -(sin_h / cos_h), sin_b)
    for q in range(PEERS):
        v_send[q] = vol_ref[:, q, :].astype(BF16)

    pl.semaphore_wait(barrier, TILES + PEERS)

    def copy(src, dst, send, recv, device):
        return pltpu.make_async_remote_copy(
            src_ref=src, dst_ref=dst, send_sem=send, recv_sem=recv, device_id=device, device_id_type=MESH
        )

    def phase_copy(o, slot):
        return copy(phase_ref, phase_all.at[slot], phase_ss.at[o], phase_rs.at[o], beside(o))

    def coef_copy(p, slot, idx):
        return copy(coef_send, coef_all.at[slot], coef_ss.at[p], coef_rs.at[idx], peer(p))

    def v_copy(p, slot, idx):
        return copy(v_send.at[slot_of(p)], v_all.at[slot, core], v_ss.at[p], v_rs.at[idx], peer(p))

    def b_copy(p, slot, idx):
        return copy(b_send.at[slot_of(p)], b_all.at[slot, core], b_ss.at[p], b_rs.at[idx], peer(p))

    def g_copy(o, slot):
        return copy(g_send.at[(tile + o) % TILES], g_all.at[slot], g_ss.at[o], g_rs.at[o], beside(o))

    def l_copy(p, slot, idx):
        return copy(l_send.at[slot_of(p)], l_all.at[slot], l_ss.at[p], l_rs.at[idx], peer(p))

    def old_copy(p, slot, idx):
        return copy(old_send.at[p], old_all.at[slot], old_ss.at[p], old_rs.at[idx], peer(p))

    def new_copy(p, slot, idx):
        return copy(new_send.at[p], new_all.at[slot], new_ss.at[p], new_rs.at[idx], peer(p))

    def k_copy(p, slot, idx):
        return copy(k_send.at[p], k_all.at[slot], k_ss.at[p], k_rs.at[idx], peer(p))

    v_twin = copy(v_all.at[:, core], v_all.at[:, core], one_ss.at[0], one_rs.at[0], twin)
    b_twin = copy(b_all.at[:, core], b_all.at[:, core], one_ss.at[1], one_rs.at[1], twin)
    s_twin = copy(s_send, s_recv, one_ss.at[2], one_rs.at[2], twin)
    halo_up = copy(v_send.at[PEERS - 1], halo.at[0], one_ss.at[3], one_rs.at[3], beside(1))
    halo_down = copy(v_send.at[0], halo.at[1], one_ss.at[4], one_rs.at[4], beside(TILES - 1))

    for o in range(1, TILES):
        phase_copy(o, tile).start()
    for p in range(PEERS):
        coef_copy(p, mine, mine).start()
    for p in range(PEERS):
        v_copy(p, mine, mine).start()
    halo_up.start()
    halo_down.start()
    phase_all[tile] = phase_ref[...]

    for p in range(PEERS):
        coef_copy(p, p, p).wait_recv()

    lane = lax.broadcasted_iota(jnp.int32, (N, HALF), 1)
    line = lax.broadcasted_iota(jnp.int32, (N, HALF), 0)
    freq_a = jnp.where(lane == 0, HALF, lane).astype(F32) * (1.0 / N)
    row_a = (line - HALF).astype(F32)
    lane_b = lax.broadcasted_iota(jnp.int32, (HALF, N), 1)
    line_b = lax.broadcasted_iota(jnp.int32, (HALF, N), 0)
    freq_b = jnp.where(line_b == 0, HALF, line_b).astype(F32) * (1.0 / N)
    row_b = (lane_b - HALF).astype(F32)

    def angle_tables(p, carry):
        coef = coef_all[p]
        shift = coef[0:1, :]
        sin, cos = sincos_turns((row_a * shift) * freq_a)
        tab_a[p, 0] = jnp.where(lane == 0, 1.0, cos)
        tab_a[p, 1] = jnp.where(lane == 0, 0.0, sin)
        tab_a[p, 2] = cos
        shift = jnp.concatenate([coef[4:5, :], coef[4:5, :]], axis=1)
        sin, cos = sincos_turns((row_b * shift) * freq_b)
        tab_b[p, 0] = jnp.where(line_b == 0, 1.0, cos)
        tab_b[p, 1] = jnp.where(line_b == 0, 0.0, sin)
        tab_b[p, 2] = cos
        return carry

    lax.fori_loop(0, PEERS, angle_tables, 0)

    for o in range(1, TILES):
        phase_copy(o, (tile + TILES - o) % TILES).wait_recv()

    sin, cos = sincos_turns(phase_all[...].reshape(BAND_ROWS, N) * (1.0 / (2.0 * math.pi)))
    parts = []
    for s in range(SHOTS):
        back = (N - offsets_ref[0, s]) % N
        c, n = pltpu.roll(cos, back, 1)[:, :HALF], pltpu.roll(sin, back, 1)[:, :HALF]
        wave_r = pr_ref[...] * c - pi_ref[...] * n
        wave_i = pr_ref[...] * n + pi_ref[...] * c
        wave[s, 0] = wave_r
        wave[s, 1] = wave_i
        parts.append(jnp.concatenate([wave_r, wave_i], axis=1).astype(BF16))
    half = dot(jnp.concatenate(parts, axis=0), near).astype(BF16)
    beams = [half[s * HALF : (s + 1) * HALF] for s in range(SHOTS)]
    beams = [jnp.concatenate([b[:, :HALF], b[:, HALF:]], axis=0) for b in beams]
    far = dot(away, jnp.concatenate(beams, axis=1))
    far_r, far_i = far[:HALF], far[HALF:]
    measured = jnp.concatenate([inten_ref[s] for s in range(SHOTS)], axis=1)
    misfit = far_r * far_r + far_i * far_i - measured
    weighted = jnp.concatenate([misfit * far_r, misfit * far_i], axis=0).astype(BF16)
    half = dot(near, weighted).astype(BF16)
    beams = [half[:, s * HALF : (s + 1) * HALF] for s in range(SHOTS)]
    beams = [jnp.concatenate([b[:HALF], b[HALF:]], axis=1) for b in beams]
    leave = dot(jnp.concatenate(beams, axis=0), away)
    image = jnp.zeros((BAND_ROWS, N), F32)
    for s in range(SHOTS):
        e = leave[s * HALF : (s + 1) * HALF]
        term = 2.0 * (e[:, HALF:] * wave[s, 0] - e[:, :HALF] * wave[s, 1])
        wide = jnp.concatenate([term, jnp.zeros((BAND_ROWS, N - HALF), F32)], axis=1)
        image = image + pltpu.roll(wide, offsets_ref[0, s], 1)
    g_send[...] = image.reshape(TILES, 8, N).astype(BF16)
    for o in range(1, TILES):
        g_copy(o, tile).start()
    g_all[tile] = g_send[tile]

    for p in range(PEERS):
        v_copy(p, p, p).wait_recv()
    v_twin.start()
    halo_up.wait_recv()
    halo_down.wait_recv()
    lower = jnp.where(tile > 0, halo[0].astype(F32), 0.0)
    upper = jnp.where(tile < TILES - 1, halo[1].astype(F32), 0.0)
    for q in range(PEERS):
        here = vol_ref[:, q, :]
        before = lower if q == 0 else vol_ref[:, q - 1, :]
        after = upper if q == PEERS - 1 else vol_ref[:, q + 1, :]
        value = here - (tau_step * smooth_weight) * (2.0 * here - before - after)
        b_own[q] = value
        b_send[q] = value.astype(BF16)
    for p in range(PEERS):
        b_copy(p, mine, mine).start()
    copy(v_all.at[:, 1 - core], v_all.at[:, 1 - core], one_ss.at[0], one_rs.at[0], twin).wait_recv()
    xs[...] = dot(v_all[...].reshape(N, N), fwd_x)

    def turned(p_part, q_part, table, p, sign):
        cos, sin, end = table[p, 0], table[p, 1], table[p, 2]
        if sign > 0:
            return p_part * cos + q_part * sin, q_part * end - p_part * sin
        return p_part * cos - q_part * sin, q_part * end + p_part * sin

    def sheared_y(u, p, sign):
        y = dot(fwd_y, u)
        turn = turned(y[:HALF], y[HALF:], tab_b, p, sign)
        return dot(inv_y, jnp.concatenate(turn, axis=0).astype(BF16)).astype(BF16)

    def project(p, carry):
        turn = turned(xs[:, :HALF], xs[:, HALF:], tab_a, p, 1)
        u = dot(jnp.concatenate(turn, axis=1).astype(BF16), inv_x).astype(BF16)
        y = dot(sheared_y(u, p, 1), fwd_x)
        turn = turned(y[:, :HALF], y[:, HALF:], tab_a, p, 1)
        spec[pl.ds(p, 1), :] = jnp.sum(jnp.concatenate(turn, axis=1), axis=0, keepdims=True)
        return carry

    lax.fori_loop(0, PEERS, project, 0)
    old = dot_parts(spec[...], inv_x) * (1.0 / math.sqrt(N))
    for p in range(PEERS):
        old_send[p] = old[p : p + 1]
    for p in range(PEERS):
        old_copy(p, my_slot, my_slot).start()

    for o in range(1, TILES):
        g_copy(o, (tile + TILES - o) % TILES).wait_recv()
    grad = jnp.sum(g_all[...].astype(F32), axis=0)
    base = phase_ref[...] - eta_step * (grad + dual_ref[...] + rho_weight * phase_ref[...])
    lines = rho_weight * base + dual_ref[...]
    for q in range(PEERS):
        l_send[q] = lines[q : q + 1]
    for p in range(PEERS):
        l_copy(p, mine, mine).start()

    for p in range(PEERS):
        b_copy(p, p, p).wait_recv()
    b_twin.start()
    copy(b_all.at[:, 1 - core], b_all.at[:, 1 - core], one_ss.at[1], one_rs.at[1], twin).wait_recv()
    xb[...] = dot(b_all[...].reshape(N, N), fwd_x)

    for p in range(PEERS):
        l_copy(p, p, p).wait_recv()
    asked = jnp.concatenate([l_all[p] for p in range(PEERS)], axis=0)
    resid = (rho_weight * (1.0 - eta_step * rho_weight)) * old - asked
    spec[...] = dot_parts(resid, fwd_x) * (1.0 / math.sqrt(N))
    s_sum[...] = jnp.zeros((N, N), F32)

    def backproject(p, carry):
        g = spec[pl.ds(p, 1), :]
        turn = turned(g[:, :HALF], g[:, HALF:], tab_a, p, -1)
        u = dot(jnp.concatenate(turn, axis=1).astype(BF16), inv_x).astype(BF16)
        y = dot(sheared_y(u, p, -1), fwd_x)
        turn = turned(y[:, :HALF], y[:, HALF:], tab_a, p, -1)
        s_sum[...] += jnp.concatenate(turn, axis=1)
        return carry

    lax.fori_loop(0, PEERS, backproject, 0)
    s_send[...] = s_sum[...].astype(BF16)
    s_twin.start()
    s_twin.wait_recv()
    total = s_sum[...] + s_recv[...].astype(F32)
    xs[...] = xb[...] - tau_step * total
    blocks = total.astype(BF16).reshape(PEERS, 2, ROWS, N)
    blocks = jnp.where(core == 0, blocks[:, 0], blocks[:, 1]).reshape(HALF, N)
    k_send[...] = dot(blocks, inv_x).astype(BF16).reshape(PEERS, ROWS, N)
    for p in range(PEERS):
        k_copy(p, my_slot, my_slot).start()

    lax.fori_loop(0, PEERS, project, 0)
    new = dot_parts(spec[...], inv_x) * (1.0 / math.sqrt(N))
    for p in range(PEERS):
        new_send[p] = new[p : p + 1]
    for p in range(PEERS):
        new_copy(p, my_slot, my_slot).start()

    for p in range(PEERS):
        k_copy(p, slot_of(p), slot_of(p)).wait_recv()
    for q in range(PEERS):
        vol_out[:, q, :] = b_own[q] - tau_step * k_all[q].astype(F32)
    for p in range(PEERS):
        old_copy(p, slot_of(p), slot_of(p)).wait_recv()
    phase_new = base + (eta_step * rho_weight) * jnp.concatenate([old_all[q] for q in range(PEERS)], axis=0)
    phase_out[...] = phase_new
    for p in range(PEERS):
        new_copy(p, slot_of(p), slot_of(p)).wait_recv()
    after = jnp.concatenate([new_all[q] for q in range(PEERS)], axis=0)
    dual_out[...] = dual_ref[...] + rho_weight * (phase_new - after)

    for o in range(1, TILES):
        phase_copy(o, tile).wait_send()
        g_copy(o, tile).wait_send()
    for p in range(PEERS):
        coef_copy(p, mine, mine).wait_send()
        v_copy(p, mine, mine).wait_send()
        b_copy(p, mine, mine).wait_send()
        l_copy(p, mine, mine).wait_send()
        old_copy(p, my_slot, my_slot).wait_send()
        new_copy(p, my_slot, my_slot).wait_send()
        k_copy(p, my_slot, my_slot).wait_send()
    for one in (v_twin, b_twin, s_twin, halo_up, halo_down):
        one.wait_send()


BAND_ROWS = 128


def shards(volume, phase, dual, probe_real, probe_imag, intensity, offsets, angle_index):
    tables = jnp.asarray(packed_tables()).astype(BF16)
    in_vmem = pl.BlockSpec(memory_space=pltpu.VMEM)
    in_smem = pl.BlockSpec(memory_space=pltpu.SMEM)
    dma = pltpu.SemaphoreType.DMA
    vmem = pltpu.VMEM
    blocks = (PEERS, ROWS, N)
    lines = (PEERS, 1, N)
    phase_new, volume_new, dual_new = pl.pallas_call(
        step_kernel,
        out_shape=(
            jax.ShapeDtypeStruct(phase.shape[1:], F32),
            jax.ShapeDtypeStruct(volume.shape, F32),
            jax.ShapeDtypeStruct(dual.shape[1:], F32),
        ),
        in_specs=[in_smem] * 2 + [in_vmem] * 7,
        out_specs=(in_vmem,) * 3,
        scratch_shapes=[
            vmem((8, 128), F32),
            vmem((PEERS, 8, 128), F32),
            vmem(blocks, BF16),
            vmem((PEERS, 2, ROWS, N), BF16),
            vmem(blocks, BF16),
            vmem((PEERS, 2, ROWS, N), BF16),
            vmem(blocks, F32),
            vmem((2, ROWS, N), BF16),
            vmem((TILES, 8, N), F32),
            vmem((TILES, 8, N), BF16),
            vmem((TILES, 8, N), BF16),
            vmem(lines, F32),
            vmem(lines, F32),
            vmem(lines, F32),
            vmem(lines, F32),
            vmem(lines, F32),
            vmem(lines, F32),
            vmem(blocks, BF16),
            vmem(blocks, BF16),
            vmem((N, N), BF16),
            vmem((N, N), BF16),
            vmem((PEERS, 3, N, HALF), F32),
            vmem((PEERS, 3, HALF, N), F32),
            vmem((N, N), F32),
            vmem((N, N), F32),
            vmem((N, N), F32),
            vmem((PEERS, N), F32),
            vmem((SHOTS, 2, HALF, HALF), F32),
            dma((TILES,)),
            dma((TILES,)),
            dma((TILES,)),
            dma((TILES,)),
        ]
        + [dma((PEERS,))] * 14
        + [dma((5,))] * 2,
        compiler_params=pltpu.CompilerParams(collective_id=0, has_side_effects=True),
    )(offsets, angle_index, volume, phase[0], dual[0], probe_real, probe_imag, intensity[0], tables)
    return (phase_new[None], volume_new, dual_new[None])


def solution(mesh):
    placed = (
        P("ang", "tile", None),
        P("ang", "tile", None),
        P("ang", "tile", None),
        P(),
        P(),
        P("ang", "tile", None, None),
        P("ang", "tile"),
        P("ang"),
    )
    return jax.shard_map(
        shards,
        mesh=mesh,
        in_specs=placed,
        out_specs=(P("ang", "tile", None), P("ang", "tile", None), P("ang", "tile", None)),
        check_vma=False,
    )
```

profile of v0, /device:TPU:1, one launch (start us, length us, event | category | flops | bytes accessed | tf_op | source)
XLA Modules:
  0.0 60.1 jit_solution(11074638432842354599)
XLA Ops:
  1.3 55.3 %shard_map.112 = (f32[8,256]{1,0:T(8,128)}, f32[16,8,256]{2,1,0:T(8,128)}, f32[8,256]{1,0:T(8,128)}) custom-call(s32[1,4]{1,0:T(1,128)} %offsets_ref.1, s32[1]{0:T(128)S(6)} %copy.15.angle_ref, f32[16,8,256]{2,1,0:T(8,128)} %vol_ref.1, f32[8,256]{1,0:T(8,128)} %bitcast.6, f32[8,256]{1,0:T(8,128)} %bitcast.7, f32[128,128]{1,0:T(8,128)} %pr_ref.1, ...), custom_call_target="tpu_custom_call" | custom-call | tf_op jit(solution)/shard_map/pallas_call | solution.py:376
  56.6 0.0 copy-start.1
  56.6 0.7 %copy-done.1 = f32[8,256]{1,0:T(8,128)S(1)} copy-done((f32[8,256]{1,0:T(8,128)S(1)}, f32[8,256]{1,0:T(8,128)}, u32[]{:S(2)}) %copy-start.1) | copy-done | bytes 8216
  57.3 0.6 copy.16
  57.9 0.0 copy-start
  57.9 1.6 %copy.17 = f32[16,8,256]{2,1,0:T(8,128)} copy(f32[16,8,256]{2,1,0:T(8,128)} %get-tuple-element.13) | data formatting | bytes 262144
  59.5 0.0 copy-done
  59.5 0.6 copy.18
Async XLA Ops:
  56.6 0.7 %copy-start.1 = (f32[8,256]{1,0:T(8,128)S(1)}, f32[8,256]{1,0:T(8,128)}, u32[]{:S(2)}) copy-start(f32[8,256]{1,0:T(8,128)} %get-tuple-element.6) | copy-start | bytes 24580
  57.9 1.6 %copy-start = (f32[8,256]{1,0:T(8,128)S(1)}, f32[8,256]{1,0:T(8,128)}, u32[]{:S(2)}) copy-start(f32[8,256]{1,0:T(8,128)} %get-tuple-element.8) | copy-start | bytes 24580
where the time goes:
time: 60.2 us; the launch traced here: 60.1 us
  Pallas kernels  55.3 us (92%)
  local copies, waits for them, and re-layouts  3.47 us (6%)
  between operations  1.3 us (2%)
    pallas_call x1, Pallas kernels, shards(): pl.pallas_call(step_kernel, out_shape=(jax.ShapeDtypeStruct(phase.shape[1...  55.3 us
    unnamed x7, local copies, waits for them, and re-layouts  3.47 us

commit v1 on v0

--- a/solution.py
+++ b/solution.py
@@ -20,6 +20,9 @@
 TILES = 16
 ROWS = 16
 SHOTS = 4
+BAND_ROWS = 128
+EARLY = 6
+NEAR_LAST = [4 * dy + dz for dy in (2, 1, 3, 0) for dz in range(4) if dy or dz]
 F32 = jnp.float32
 BF16 = jnp.bfloat16
 MESH = pl.DeviceIdType.MESH
@@ -78,13 +81,14 @@
 
 
 def step_kernel(
-    offsets_ref, angle_ref, vol_ref, phase_ref, dual_ref, pr_ref, pi_ref, inten_ref, tab_ref,
+    offsets_in, angle_in, vol_in, phase_in, dual_in, pr_in, pi_in, inten_in, tab_in,
     phase_out, vol_out, dual_out,
+    offsets_ref, angle_ref, vol_ref, phase_ref, dual_ref, pr_ref, pi_ref, inten_ref, tab_ref, phase_send,
     coef_send, coef_all, v_send, v_all, b_send, b_all, b_own, halo, phase_all, g_send, g_all, l_send, l_all,
     old_send, old_all, new_send, new_all, k_send, k_all, s_send, s_recv,
-    tab_a, tab_b, xs, xb, s_sum, spec, wave,
+    tab_a, tab_b, xs, xb, s_sum, wave,
     phase_ss, phase_rs, g_ss, g_rs, coef_ss, coef_rs, v_ss, v_rs, b_ss, b_rs, l_ss, l_rs,
-    old_ss, old_rs, new_ss, new_rs, k_ss, k_rs, one_ss, one_rs,
+    old_ss, old_rs, new_ss, new_rs, k_ss, k_rs, one_ss, one_rs, in_sem,
 ):
     me = lax.axis_index("ang")
     tile = lax.axis_index("tile")
@@ -105,22 +109,42 @@
         return 2 * (p // 2) + (p % 2 + turn_out) % 2
 
     def beside(o):
-        return (me, (tile + o) % TILES)
+        return (me, ((tile // 4 + o // 4) % 4) * 4 + (low + o) % 4)
+
+    def sender(o):
+        return ((tile // 4 + 4 - o // 4) % 4) * 4 + (low + 4 - o % 4) % 4
+
+    order = [2 * ((x_me + dx) % 4) + zh for dx in (2, 1, 3, 0) for zh in (0, 1)]
 
     barrier = pltpu.get_barrier_semaphore()
-    for o in range(1, TILES):
+    for o in NEAR_LAST:
         pl.semaphore_signal(barrier, inc=1, device_id=beside(o), device_id_type=MESH)
     for p in range(PEERS):
         pl.semaphore_signal(barrier, inc=1, device_id=peer(p), device_id_type=MESH)
     pl.semaphore_signal(barrier, inc=1, device_id=twin, device_id_type=MESH)
 
-    fwd_x, inv_x, fwd_y, inv_y, near, away = (tab_ref[i] for i in range(6))
-
+    loads = [
+        pltpu.make_async_copy(src, dst, in_sem.at[i])
+        for i, (src, dst) in enumerate(
+            [
+                (angle_in, angle_ref), (phase_in, phase_ref), (vol_in, vol_ref), (offsets_in, offsets_ref),
+                (pr_in, pr_ref), (pi_in, pi_ref), (inten_in, inten_ref), (tab_in, tab_ref), (dual_in, dual_ref),
+            ]
+        )
+    ]
+    for load in loads:
+        load.start()
+
+    loads[0].wait()
     number = jnp.full((8, 128), angle_ref[0], jnp.int32).astype(F32) - angle_center
     sin_b, unused = sincos_turns(number * (1.0 / 720.0))
     sin_h, cos_h = sincos_turns(number * (1.0 / 1440.0))
     rows8 = lax.broadcasted_iota(jnp.int32, (8, 128), 0)
     coef_send[...] = jnp.where(rows8 < 4, -(sin_h / cos_h), sin_b)
+    loads[1].wait()
+    turns = phase_ref[...] * (1.0 / (2.0 * math.pi))
+    phase_send[...] = (turns - jnp.floor(turns + 0.5)).astype(BF16)
+    loads[2].wait()
     for q in range(PEERS):
         v_send[q] = vol_ref[:, q, :].astype(BF16)
 
@@ -132,7 +156,7 @@
         )
 
     def phase_copy(o, slot):
-        return copy(phase_ref, phase_all.at[slot], phase_ss.at[o], phase_rs.at[o], beside(o))
+        return copy(phase_send, phase_all.at[slot], phase_ss.at[o], phase_rs.at[o], beside(o))
 
     def coef_copy(p, slot, idx):
         return copy(coef_send, coef_all.at[slot], coef_ss.at[p], coef_rs.at[idx], peer(p))
@@ -144,16 +168,16 @@
         return copy(b_send.at[slot_of(p)], b_all.at[slot, core], b_ss.at[p], b_rs.at[idx], peer(p))
 
     def g_copy(o, slot):
-        return copy(g_send.at[(tile + o) % TILES], g_all.at[slot], g_ss.at[o], g_rs.at[o], beside(o))
+        return copy(g_send.at[beside(o)[1]], g_all.at[slot], g_ss.at[o], g_rs.at[o], beside(o))
 
     def l_copy(p, slot, idx):
         return copy(l_send.at[slot_of(p)], l_all.at[slot], l_ss.at[p], l_rs.at[idx], peer(p))
 
-    def old_copy(p, slot, idx):
-        return copy(old_send.at[p], old_all.at[slot], old_ss.at[p], old_rs.at[idx], peer(p))
-
-    def new_copy(p, slot, idx):
-        return copy(new_send.at[p], new_all.at[slot], new_ss.at[p], new_rs.at[idx], peer(p))
+    def old_copy(j, p, slot, idx):
+        return copy(old_send.at[j], old_all.at[slot], old_ss.at[j], old_rs.at[idx], peer(p))
+
+    def new_copy(j, p, slot, idx):
+        return copy(new_send.at[j], new_all.at[slot], new_ss.at[j], new_rs.at[idx], peer(p))
 
     def k_copy(p, slot, idx):
         return copy(k_send.at[p], k_all.at[slot], k_ss.at[p], k_rs.at[idx], peer(p))
@@ -161,18 +185,21 @@
     v_twin = copy(v_all.at[:, core], v_all.at[:, core], one_ss.at[0], one_rs.at[0], twin)
     b_twin = copy(b_all.at[:, core], b_all.at[:, core], one_ss.at[1], one_rs.at[1], twin)
     s_twin = copy(s_send, s_recv, one_ss.at[2], one_rs.at[2], twin)
-    halo_up = copy(v_send.at[PEERS - 1], halo.at[0], one_ss.at[3], one_rs.at[3], beside(1))
-    halo_down = copy(v_send.at[0], halo.at[1], one_ss.at[4], one_rs.at[4], beside(TILES - 1))
-
-    for o in range(1, TILES):
+    halo_up = copy(v_send.at[PEERS - 1], halo.at[0], one_ss.at[3], one_rs.at[3], (me, (tile + 1) % TILES))
+    halo_down = copy(v_send.at[0], halo.at[1], one_ss.at[4], one_rs.at[4], (me, (tile + TILES - 1) % TILES))
+
+    for p in range(PEERS):
+        coef_copy(p, mine, mine).start()
+    for o in NEAR_LAST:
         phase_copy(o, tile).start()
-    for p in range(PEERS):
-        coef_copy(p, mine, mine).start()
     for p in range(PEERS):
         v_copy(p, mine, mine).start()
     halo_up.start()
     halo_down.start()
-    phase_all[tile] = phase_ref[...]
+    phase_all[tile] = phase_send[...]
+    for load in loads[3:]:
+        load.wait()
+    fwd_x, inv_x, fwd_y, inv_y, near, away = (tab_ref[i] for i in range(6))
 
     for p in range(PEERS):
         coef_copy(p, p, p).wait_recv()
@@ -203,9 +230,9 @@
     lax.fori_loop(0, PEERS, angle_tables, 0)
 
     for o in range(1, TILES):
-        phase_copy(o, (tile + TILES - o) % TILES).wait_recv()
-
-    sin, cos = sincos_turns(phase_all[...].reshape(BAND_ROWS, N) * (1.0 / (2.0 * math.pi)))
+        phase_copy(o, sender(o)).wait_recv()
+
+    sin, cos = sincos_turns(phase_all[...].astype(F32).reshape(BAND_ROWS, N))
     parts = []
     for s in range(SHOTS):
         back = (N - offsets_ref[0, s]) % N
@@ -234,7 +261,7 @@
         wide = jnp.concatenate([term, jnp.zeros((BAND_ROWS, N - HALF), F32)], axis=1)
         image = image + pltpu.roll(wide, offsets_ref[0, s], 1)
     g_send[...] = image.reshape(TILES, 8, N).astype(BF16)
-    for o in range(1, TILES):
+    for o in NEAR_LAST:
         g_copy(o, tile).start()
     g_all[tile] = g_send[tile]
 
@@ -268,23 +295,20 @@
         turn = turned(y[:HALF], y[HALF:], tab_b, p, sign)
         return dot(inv_y, jnp.concatenate(turn, axis=0).astype(BF16)).astype(BF16)
 
-    def project(p, carry):
+    def project(p):
         turn = turned(xs[:, :HALF], xs[:, HALF:], tab_a, p, 1)
         u = dot(jnp.concatenate(turn, axis=1).astype(BF16), inv_x).astype(BF16)
         y = dot(sheared_y(u, p, 1), fwd_x)
         turn = turned(y[:, :HALF], y[:, HALF:], tab_a, p, 1)
-        spec[pl.ds(p, 1), :] = jnp.sum(jnp.concatenate(turn, axis=1), axis=0, keepdims=True)
-        return carry
-
-    lax.fori_loop(0, PEERS, project, 0)
-    old = dot_parts(spec[...], inv_x) * (1.0 / math.sqrt(N))
-    for p in range(PEERS):
-        old_send[p] = old[p : p + 1]
-    for p in range(PEERS):
-        old_copy(p, my_slot, my_slot).start()
+        return jnp.sum(jnp.concatenate(turn, axis=1), axis=0, keepdims=True)
+
+    def lines_of(spectra):
+        return dot_parts(jnp.concatenate(spectra, axis=0), inv_x) * (1.0 / math.sqrt(N))
+
+    spectra = [project(p) for p in order[:EARLY]]
 
     for o in range(1, TILES):
-        g_copy(o, (tile + TILES - o) % TILES).wait_recv()
+        g_copy(o, sender(o)).wait_recv()
     grad = jnp.sum(g_all[...].astype(F32), axis=0)
     base = phase_ref[...] - eta_step * (grad + dual_ref[...] + rho_weight * phase_ref[...])
     lines = rho_weight * base + dual_ref[...]
@@ -296,26 +320,32 @@
     for p in range(PEERS):
         b_copy(p, p, p).wait_recv()
     b_twin.start()
+    spectra += [project(p) for p in order[EARLY:]]
+    old = lines_of(spectra)
+    for j, p in enumerate(order):
+        old_send[j] = old[j : j + 1]
+    for j, p in enumerate(order):
+        old_copy(j, p, my_slot, my_slot).start()
     copy(b_all.at[:, 1 - core], b_all.at[:, 1 - core], one_ss.at[1], one_rs.at[1], twin).wait_recv()
     xb[...] = dot(b_all[...].reshape(N, N), fwd_x)
 
     for p in range(PEERS):
         l_copy(p, p, p).wait_recv()
-    asked = jnp.concatenate([l_all[p] for p in range(PEERS)], axis=0)
+    asked = jnp.concatenate([l_all[p] for p in order], axis=0)
     resid = (rho_weight * (1.0 - eta_step * rho_weight)) * old - asked
-    spec[...] = dot_parts(resid, fwd_x) * (1.0 / math.sqrt(N))
+    asked = dot_parts(resid, fwd_x) * (1.0 / math.sqrt(N))
     s_sum[...] = jnp.zeros((N, N), F32)
 
-    def backproject(p, carry):
-        g = spec[pl.ds(p, 1), :]
+    def backproject(j, p):
+        g = asked[j : j + 1]
         turn = turned(g[:, :HALF], g[:, HALF:], tab_a, p, -1)
         u = dot(jnp.concatenate(turn, axis=1).astype(BF16), inv_x).astype(BF16)
         y = dot(sheared_y(u, p, -1), fwd_x)
         turn = turned(y[:, :HALF], y[:, HALF:], tab_a, p, -1)
         s_sum[...] += jnp.concatenate(turn, axis=1)
-        return carry
-
-    lax.fori_loop(0, PEERS, backproject, 0)
+
+    for j, p in enumerate(order):
+        backproject(j, p)
     s_send[...] = s_sum[...].astype(BF16)
     s_twin.start()
     s_twin.wait_recv()
@@ -327,23 +357,23 @@
     for p in range(PEERS):
         k_copy(p, my_slot, my_slot).start()
 
-    lax.fori_loop(0, PEERS, project, 0)
-    new = dot_parts(spec[...], inv_x) * (1.0 / math.sqrt(N))
-    for p in range(PEERS):
-        new_send[p] = new[p : p + 1]
-    for p in range(PEERS):
-        new_copy(p, my_slot, my_slot).start()
+    for first, last in ((0, 2), (2, 6), (6, 8)):
+        new = lines_of([project(p) for p in order[first:last]])
+        for j in range(first, last):
+            new_send[j] = new[j - first : j - first + 1]
+        for j in range(first, last):
+            new_copy(j, order[j], my_slot, my_slot).start()
 
     for p in range(PEERS):
         k_copy(p, slot_of(p), slot_of(p)).wait_recv()
     for q in range(PEERS):
         vol_out[:, q, :] = b_own[q] - tau_step * k_all[q].astype(F32)
     for p in range(PEERS):
-        old_copy(p, slot_of(p), slot_of(p)).wait_recv()
+        old_copy(p, p, slot_of(p), slot_of(p)).wait_recv()
     phase_new = base + (eta_step * rho_weight) * jnp.concatenate([old_all[q] for q in range(PEERS)], axis=0)
     phase_out[...] = phase_new
     for p in range(PEERS):
-        new_copy(p, slot_of(p), slot_of(p)).wait_recv()
+        new_copy(p, p, slot_of(p), slot_of(p)).wait_recv()
     after = jnp.concatenate([new_all[q] for q in range(PEERS)], axis=0)
     dual_out[...] = dual_ref[...] + rho_weight * (phase_new - after)
 
@@ -355,34 +385,48 @@
         v_copy(p, mine, mine).wait_send()
         b_copy(p, mine, mine).wait_send()
         l_copy(p, mine, mine).wait_send()
-        old_copy(p, my_slot, my_slot).wait_send()
-        new_copy(p, my_slot, my_slot).wait_send()
+        old_copy(p, order[p], my_slot, my_slot).wait_send()
+        new_copy(p, order[p], my_slot, my_slot).wait_send()
         k_copy(p, my_slot, my_slot).wait_send()
     for one in (v_twin, b_twin, s_twin, halo_up, halo_down):
         one.wait_send()
 
 
-BAND_ROWS = 128
+def hand_over(phase_in, vol_in, dual_in, phase_out, vol_out, dual_out):
+    phase_out[...] = phase_in[...]
+    vol_out[...] = vol_in[...]
+    dual_out[...] = dual_in[...]
 
 
 def shards(volume, phase, dual, probe_real, probe_imag, intensity, offsets, angle_index):
     tables = jnp.asarray(packed_tables()).astype(BF16)
     in_vmem = pl.BlockSpec(memory_space=pltpu.VMEM)
-    in_smem = pl.BlockSpec(memory_space=pltpu.SMEM)
+    in_place = pl.BlockSpec(memory_space=pl.ANY)
     dma = pltpu.SemaphoreType.DMA
     vmem = pltpu.VMEM
     blocks = (PEERS, ROWS, N)
     lines = (PEERS, 1, N)
-    phase_new, volume_new, dual_new = pl.pallas_call(
+    results = (
+        jax.ShapeDtypeStruct(phase.shape[1:], F32),
+        jax.ShapeDtypeStruct(volume.shape, F32),
+        jax.ShapeDtypeStruct(dual.shape[1:], F32),
+    )
+    made = pl.pallas_call(
         step_kernel,
-        out_shape=(
-            jax.ShapeDtypeStruct(phase.shape[1:], F32),
-            jax.ShapeDtypeStruct(volume.shape, F32),
-            jax.ShapeDtypeStruct(dual.shape[1:], F32),
-        ),
-        in_specs=[in_smem] * 2 + [in_vmem] * 7,
+        out_shape=results,
+        in_specs=[in_place] * 9,
         out_specs=(in_vmem,) * 3,
         scratch_shapes=[
+            pltpu.SMEM((1, SHOTS), jnp.int32),
+            pltpu.SMEM((1,), jnp.int32),
+            vmem(volume.shape, F32),
+            vmem((8, N), F32),
+            vmem((8, N), F32),
+            vmem((HALF, HALF), F32),
+            vmem((HALF, HALF), F32),
+            vmem((SHOTS, HALF, HALF), F32),
+            vmem(tables.shape, BF16),
+            vmem((8, N), BF16),
             vmem((8, 128), F32),
             vmem((PEERS, 8, 128), F32),
             vmem(blocks, BF16),
@@ -391,7 +435,7 @@
             vmem((PEERS, 2, ROWS, N), BF16),
             vmem(blocks, F32),
             vmem((2, ROWS, N), BF16),
-            vmem((TILES, 8, N), F32),
+            vmem((TILES, 8, N), BF16),
             vmem((TILES, 8, N), BF16),
             vmem((TILES, 8, N), BF16),
             vmem(lines, F32),
@@ -409,7 +453,6 @@
             vmem((N, N), F32),
             vmem((N, N), F32),
             vmem((N, N), F32),
-            vmem((PEERS, N), F32),
             vmem((SHOTS, 2, HALF, HALF), F32),
             dma((TILES,)),
             dma((TILES,)),
@@ -417,9 +460,13 @@
             dma((TILES,)),
         ]
         + [dma((PEERS,))] * 14
-        + [dma((5,))] * 2,
+        + [dma((5,))] * 2
+        + [dma((9,))],
         compiler_params=pltpu.CompilerParams(collective_id=0, has_side_effects=True),
     )(offsets, angle_index, volume, phase[0], dual[0], probe_real, probe_imag, intensity[0], tables)
+    phase_new, volume_new, dual_new = pl.pallas_call(
+        hand_over, out_shape=results, in_specs=[in_vmem] * 3, out_specs=(in_vmem,) * 3
+    )(*made)
     return (phase_new[None], volume_new, dual_new[None])
 
 

time: 60.2 us -> 49.9 us (0.83)
  Pallas kernels: 55.3 us -> 48.5 us
  local copies, waits for them, and re-layouts: 3.47 us -> 0 us
    pallas_call x1 -> x2, Pallas kernels: 55.3 us -> 48.5 us  [the longest x1 46.9 us: shards(): pl.pallas_call(step_kernel, out_shape=results, in_specs=[in_place] * 9, o...]
    unnamed x7 -> x0, local copies, waits for them, and re-layouts: 3.47 us -> none
where the time goes in v1:
time: 49.9 us; the launch traced here: 49.7 us
  Pallas kernels  48.5 us (97%)
  between operations  1.29 us (3%)
    pallas_call x1, Pallas kernels, shards(): pl.pallas_call(step_kernel, out_shape=results, in_specs=[in_place] * 9, o...  46.9 us
    pallas_call x1, Pallas kernels, shards(): pl.pallas_call(hand_over, out_shape=results, in_specs=[in_vmem] * 3, out_...  1.57 us

profile of v1, /device:TPU:1, one launch (start us, length us, event | category | flops | bytes accessed | tf_op | source)
XLA Modules:
  0.0 49.7 jit_solution(3751843303310698333)
XLA Ops:
  1.3 46.9 %shard_map.112 = (f32[8,256]{1,0:T(8,128)}, f32[16,8,256]{2,1,0:T(8,128)}, f32[8,256]{1,0:T(8,128)}) custom-call(s32[1,4]{1,0:T(1,128)} %offsets_in.1, s32[1]{0:T(128)S(6)} %copy.12.angle_in, f32[16,8,256]{2,1,0:T(8,128)} %vol_in.1, f32[8,256]{1,0:T(8,128)} %bitcast.6, f32[8,256]{1,0:T(8,128)} %bitcast.7, f32[128,128]{1,0:T(8,128)} %pr_in.1, ...), custom_call_target="tpu_custom_call" | custom-call | tf_op jit(solution)/shard_map/pallas_call | solution.py:414
  48.2 1.6 %shard_map.113 = (f32[8,256]{1,0:T(8,128)}, f32[16,8,256]{2,1,0:T(8,128)}, f32[8,256]{1,0:T(8,128)}) custom-call(f32[8,256]{1,0:T(8,128)} %get-tuple-element.9.phase_in, f32[16,8,256]{2,1,0:T(8,128)} %get-tuple-element.10.vol_in, f32[8,256]{1,0:T(8,128)} %get-tuple-element.11.dual_in), custom_call_target="tpu_custom_call" | custom-call | tf_op jit(solution)/shard_map/pallas_call | solution.py:467

commit v2 on v1

v2 whole, which is shorter than its diff:
```python
import math

import jax
import jax.numpy as jnp
import numpy as np
from jax import lax
from jax.experimental import pallas as pl
from jax.experimental.pallas import tpu as pltpu
from jax.sharding import PartitionSpec as P

angle_center = 90.0
rho_weight = 1.0
eta_step = 0.01
tau_step = 1.0
smooth_weight = 0.25

N = 256
HALF = 128
PEERS = 8
TILES = 16
ROWS = 16
SHOTS = 4
BAND_ROWS = 128
STRIP = 32
FWD_X, INV_X, FWD_Y, INV_Y = range(4)
PHASE, GRAD, COEF, VOLUME, SMOOTH, LINES, OLD, NEW, BACK = range(9)
PARTS = 4
NEAR_LAST = [4 * dy + dz for dy in (2, 1, 3, 0) for dz in range(4) if dy or dz]
F32 = jnp.float32
BF16 = jnp.bfloat16
MESH = pl.DeviceIdType.MESH


def tables_of(length):
    index = np.arange(length)
    phases = (index[:, None] * index[None, :] % length).astype(np.float32)
    phases = phases * np.float32(2.0 * math.pi / length)
    return np.cos(phases), np.sin(phases)


def packed_tables():
    cos, sin = tables_of(N)
    signs = np.where(np.arange(N) % 2 == 0, 1.0, -1.0)
    forward = np.concatenate([cos[:, :HALF], -sin[:, :HALF]], axis=1)
    forward[:, HALF] = signs
    inverse = np.concatenate([2.0 * cos[:HALF], -2.0 * sin[:HALF]], axis=0)
    inverse[0] = 1.0
    inverse[HALF] = signs
    inverse = inverse / N
    cos, sin = tables_of(HALF)
    cos, sin = cos / math.sqrt(HALF), sin / math.sqrt(HALF)
    near = np.block([[cos, -sin], [sin, cos]])
    away = np.block([[cos, sin], [-sin, cos]])
    stack = np.stack([forward, inverse, forward.T, inverse.T, near, away])
    return stack.astype(np.float32)


def sincos_turns(turns):
    a = (turns - jnp.floor(turns + 0.5)) * math.pi
    z = a * a
    sin = 1.0
    for k in (12, 10, 8, 6, 4, 2):
        sin = 1.0 - z * sin * (1.0 / (k * (k + 1)))
    sin = a * sin
    cos = 1.0
    for k in (13, 11, 9, 7, 5, 3, 1):
        cos = 1.0 - z * cos * (1.0 / (k * (k + 1)))
    return 2.0 * sin * cos, 1.0 - 2.0 * sin * sin


def dot(a, b):
    return jnp.dot(a, b, preferred_element_type=F32)


def two_parts(x):
    high = x.astype(BF16)
    low = (x - high.astype(F32)).astype(BF16)
    return jnp.concatenate([high, low], axis=0)


def dot_parts(x, table):
    both = dot(two_parts(x), table)
    return both[: x.shape[0]] + both[x.shape[0] :]


def step_kernel(
    offsets_in, angle_in, vol_in, phase_in, dual_in, pr_in, pi_in, inten_in, tab_in,
    phase_out, vol_out, dual_out,
    offsets_ref, angle_ref, vol_ref, phase_ref, dual_ref, pr_ref, pi_ref, inten_ref, tab_ref, phase_send,
    coef_send, coef_all, v_send, v_all, b_send, b_all, b_own, halo, phase_all, g_send, g_all, l_send, l_all,
    old_send, old_all, new_send, new_all, k_send, k_all, s_send, s_recv,
    work_a, work_b, vol_made, phase_made, dual_made, tab_a, tab_b, xs, xb, s_sum, wave,
    sent, came, one_ss, one_rs, part_ss, part_rs, in_sem,
):
    me = lax.axis_index("ang")
    tile = lax.axis_index("tile")
    core = me % 2
    mine = me // 2
    x_me, hi_me = mine // 2, mine % 2
    low = tile % 4
    far_tile = (tile // 4) * 4 + (low + 2) % 4
    turn_out = (low + 2) // 4
    turn_in = ((low + 2) % 4 + 2) // 4
    my_slot = 2 * x_me + (hi_me + turn_in) % 2
    twin = (me - core + (1 - core), tile)

    def peer(p):
        return (2 * p + core, far_tile)

    def slot_of(p):
        return 2 * (p // 2) + (p % 2 + turn_out) % 2

    def beside(o):
        return (me, ((tile // 4 + o // 4) % 4) * 4 + (low + o) % 4)

    order = [2 * ((x_me + dx) % 4) + zh for dx in (2, 1, 3, 0) for zh in (0, 1)]

    barrier = pltpu.get_barrier_semaphore()
    for o in NEAR_LAST:
        pl.semaphore_signal(barrier, inc=1, device_id=beside(o), device_id_type=MESH)
    for p in range(PEERS):
        pl.semaphore_signal(barrier, inc=1, device_id=peer(p), device_id_type=MESH)
    pl.semaphore_signal(barrier, inc=1, device_id=twin, device_id_type=MESH)

    loads = [
        pltpu.make_async_copy(src, dst, in_sem.at[i])
        for i, (src, dst) in enumerate(
            [
                (angle_in, angle_ref), (phase_in, phase_ref), (vol_in, vol_ref), (offsets_in, offsets_ref),
                (pr_in, pr_ref), (pi_in, pi_ref), (inten_in, inten_ref), (tab_in, tab_ref), (dual_in, dual_ref),
            ]
        )
    ]
    for load in loads:
        load.start()

    loads[0].wait()
    number = jnp.full((8, 128), angle_ref[0], jnp.int32).astype(F32) - angle_center
    sin_b, unused = sincos_turns(number * (1.0 / 720.0))
    sin_h, cos_h = sincos_turns(number * (1.0 / 1440.0))
    rows8 = lax.broadcasted_iota(jnp.int32, (8, 128), 0)
    coef_send[...] = jnp.where(rows8 < 4, -(sin_h / cos_h), sin_b)
    loads[1].wait()
    turns = phase_ref[...] * (1.0 / (2.0 * math.pi))
    phase_send[...] = (turns - jnp.floor(turns + 0.5)).astype(BF16)
    loads[2].wait()
    for q in range(PEERS):
        v_send[q] = vol_ref[:, q, :].astype(BF16)

    pl.semaphore_wait(barrier, TILES + PEERS)

    def copy(src, dst, send, recv, device):
        return pltpu.make_async_remote_copy(
            src_ref=src, dst_ref=dst, send_sem=send, recv_sem=recv, device_id=device, device_id_type=MESH
        )

    def phase_copy(o, slot):
        return copy(phase_send, phase_all.at[slot], sent.at[0], came.at[0], beside(o))

    def coef_copy(p, slot):
        return copy(coef_send, coef_all.at[slot], sent.at[2], came.at[2], peer(p))

    def v_copy(p, slot):
        return copy(v_send.at[slot_of(p)], v_all.at[slot, core], sent.at[3], came.at[3], peer(p))

    def b_copy(p, slot):
        return copy(b_send.at[slot_of(p)], b_all.at[slot, core], sent.at[4], came.at[4], peer(p))

    def g_copy(o, slot):
        return copy(g_send.at[beside(o)[1]], g_all.at[slot], sent.at[1], came.at[1], beside(o))

    def l_copy(p, slot):
        return copy(l_send.at[slot_of(p)], l_all.at[slot], sent.at[5], came.at[5], peer(p))

    def old_copy(j, p, slot):
        return copy(old_send.at[j], old_all.at[slot], sent.at[6], came.at[6], peer(p))

    def new_copy(j, p, slot):
        return copy(new_send.at[j], new_all.at[slot], sent.at[7], came.at[7], peer(p))

    def k_copy(p, slot):
        return copy(k_send.at[p], k_all.at[slot], sent.at[8], came.at[8], peer(p))

    others = pl.ds(0, TILES - 1)
    groups = [phase_all.at[others], g_all.at[others], coef_all, v_send, b_send, l_send, old_send, new_send, k_send]

    def arrived(group):
        copy(groups[group], groups[group], sent.at[group], came.at[group], twin).wait_recv()

    v_twin = copy(v_all.at[:, core], v_all.at[:, core], one_ss.at[0], one_rs.at[0], twin)
    b_twin = copy(b_all.at[:, core], b_all.at[:, core], one_ss.at[1], one_rs.at[1], twin)
    parts = [slice(r, r + N // PARTS) for r in range(0, N, N // PARTS)]
    s_twins = [
        copy(s_send.at[rows], s_recv.at[rows], part_ss.at[i], part_rs.at[i], twin) for i, rows in enumerate(parts)
    ]
    halo_up = copy(v_send.at[PEERS - 1], halo.at[0], one_ss.at[2], one_rs.at[2], (me, (tile + 1) % TILES))
    halo_down = copy(v_send.at[0], halo.at[1], one_ss.at[3], one_rs.at[3], (me, (tile + TILES - 1) % TILES))

    for p in range(PEERS):
        coef_copy(p, mine).start()
    for o in NEAR_LAST:
        phase_copy(o, tile).start()
    for p in range(PEERS):
        v_copy(p, mine).start()
    halo_up.start()
    halo_down.start()
    phase_all[tile] = phase_send[...]
    for load in loads[3:]:
        load.wait()
    near, away = tab_ref[4], tab_ref[5]

    arrived(PHASE)

    sin, cos = sincos_turns(phase_all[...].astype(F32).reshape(BAND_ROWS, N))
    waves = []
    for s in range(SHOTS):
        back = (N - offsets_ref[0, s]) % N
        c, n = pltpu.roll(cos, back, 1)[:, :HALF], pltpu.roll(sin, back, 1)[:, :HALF]
        wave_r = pr_ref[...] * c - pi_ref[...] * n
        wave_i = pr_ref[...] * n + pi_ref[...] * c
        wave[s, 0] = wave_r
        wave[s, 1] = wave_i
        waves.append(jnp.concatenate([wave_r, wave_i], axis=1).astype(BF16))
    half = dot(jnp.concatenate(waves, axis=0), near).astype(BF16)
    beams = [half[s * HALF : (s + 1) * HALF] for s in range(SHOTS)]
    beams = [jnp.concatenate([b[:, :HALF], b[:, HALF:]], axis=0) for b in beams]
    far = dot(away, jnp.concatenate(beams, axis=1))
    far_r, far_i = far[:HALF], far[HALF:]
    measured = jnp.concatenate([inten_ref[s] for s in range(SHOTS)], axis=1)
    misfit = far_r * far_r + far_i * far_i - measured
    weighted = jnp.concatenate([misfit * far_r, misfit * far_i], axis=0).astype(BF16)
    half = dot(near, weighted).astype(BF16)
    beams = [half[:, s * HALF : (s + 1) * HALF] for s in range(SHOTS)]
    beams = [jnp.concatenate([b[:HALF], b[HALF:]], axis=1) for b in beams]
    leave = dot(jnp.concatenate(beams, axis=0), away)
    image = jnp.zeros((BAND_ROWS, N), F32)
    for s in range(SHOTS):
        e = leave[s * HALF : (s + 1) * HALF]
        term = 2.0 * (e[:, HALF:] * wave[s, 0] - e[:, :HALF] * wave[s, 1])
        wide = jnp.concatenate([term, jnp.zeros((BAND_ROWS, N - HALF), F32)], axis=1)
        image = image + pltpu.roll(wide, offsets_ref[0, s], 1)
    g_send[...] = image.reshape(TILES, 8, N).astype(BF16)
    for o in NEAR_LAST:
        g_copy(o, tile).start()
    g_all[tile] = g_send[tile]
    halo_up.wait_recv()
    halo_down.wait_recv()
    lower = jnp.where(tile > 0, halo[0].astype(F32), 0.0)
    upper = jnp.where(tile < TILES - 1, halo[1].astype(F32), 0.0)
    for q in range(PEERS):
        here = vol_ref[:, q, :]
        before = lower if q == 0 else vol_ref[:, q - 1, :]
        after = upper if q == PEERS - 1 else vol_ref[:, q + 1, :]
        value = here - (tau_step * smooth_weight) * (2.0 * here - before - after)
        b_own[q] = value
        b_send[q] = value.astype(BF16)
    for p in range(PEERS):
        b_copy(p, mine).start()

    arrived(COEF)

    lane = lax.broadcasted_iota(jnp.int32, (N, HALF), 1)
    line = lax.broadcasted_iota(jnp.int32, (N, HALF), 0)
    freq_a = jnp.where(lane == 0, HALF, lane).astype(F32) * (1.0 / N)
    row_a = (line - HALF).astype(F32)
    lane_b = lax.broadcasted_iota(jnp.int32, (HALF, N), 1)
    line_b = lax.broadcasted_iota(jnp.int32, (HALF, N), 0)
    freq_b = jnp.where(line_b == 0, HALF, line_b).astype(F32) * (1.0 / N)
    row_b = (lane_b - HALF).astype(F32)

    def angle_tables(p, carry):
        coef = coef_all[p]
        shift = coef[0:1, :]
        sin, cos = sincos_turns((row_a * shift) * freq_a)
        tab_a[p, 0] = jnp.where(lane == 0, 1.0, cos)
        tab_a[p, 1] = jnp.where(lane == 0, 0.0, sin)
        tab_a[p, 2] = cos
        shift = jnp.concatenate([coef[4:5, :], coef[4:5, :]], axis=1)
        sin, cos = sincos_turns((row_b * shift) * freq_b)
        tab_b[p, 0] = jnp.where(line_b == 0, 1.0, cos)
        tab_b[p, 1] = jnp.where(line_b == 0, 0.0, sin)
        tab_b[p, 2] = cos
        return carry

    lax.fori_loop(0, PEERS, angle_tables, 0)

    arrived(VOLUME)
    v_twin.start()
    copy(v_all.at[:, 1 - core], v_all.at[:, 1 - core], one_ss.at[0], one_rs.at[0], twin).wait_recv()
    xs[...] = dot(v_all[...].reshape(N, N), tab_ref[FWD_X])

    def turned(p_part, q_part, table, p, rows, sign):
        cos, sin, end = table[p, 0, rows], table[p, 1, rows], table[p, 2, rows]
        if sign > 0:
            return p_part * cos + q_part * sin, q_part * end - p_part * sin
        return p_part * cos - q_part * sin, q_part * end + p_part * sin

    whole = slice(None)

    def sheared(prepare, start, middle, sign):
        for i, part in enumerate(parts):
            prepare(i, part)
            for j, p in enumerate(order):
                for r in range(part.start, part.stop, STRIP):
                    rows = slice(r, r + STRIP)
                    first, second = start(j, rows)
                    first, second = turned(first, second, tab_a, p, rows, sign)
                    work_a[j, rows, :HALF] = first.astype(BF16)
                    work_a[j, rows, HALF:] = second.astype(BF16)
        middle()
        for j in range(PEERS):
            work_b[j] = dot(work_a[j], tab_ref[INV_X]).astype(BF16)
        for j, p in enumerate(order):
            y = dot(tab_ref[FWD_Y], work_b[j])
            first, second = turned(y[:HALF], y[HALF:], tab_b, p, whole, sign)
            work_a[j, :HALF] = first.astype(BF16)
            work_a[j, HALF:] = second.astype(BF16)
        for j in range(PEERS):
            work_b[j] = dot(tab_ref[INV_Y], work_a[j]).astype(BF16)

    def projected(prepare, middle):
        sheared(prepare, lambda j, rows: (xs[rows, :HALF], xs[rows, HALF:]), middle, 1)
        spectra = []
        for j, p in enumerate(order):
            y = dot(work_b[j], tab_ref[FWD_X])
            turn = turned(y[:, :HALF], y[:, HALF:], tab_a, p, whole, 1)
            spectra.append(jnp.sum(jnp.concatenate(turn, axis=1), axis=0, keepdims=True))
        return dot_parts(jnp.concatenate(spectra, axis=0), tab_ref[INV_X]) * (1.0 / math.sqrt(N))

    def nothing(*unused):
        pass

    arrived(GRAD)
    grad = jnp.sum(g_all[...].astype(F32), axis=0)
    base = phase_ref[...] - eta_step * (grad + dual_ref[...] + rho_weight * phase_ref[...])
    lines = rho_weight * base + dual_ref[...]
    for q in range(PEERS):
        l_send[q] = lines[q : q + 1]
    for p in range(PEERS):
        l_copy(p, mine).start()

    arrived(SMOOTH)
    b_twin.start()
    old = projected(nothing, nothing)
    for j, p in enumerate(order):
        old_send[j] = old[j : j + 1]
    for j, p in enumerate(order):
        old_copy(j, p, my_slot).start()
    copy(b_all.at[:, 1 - core], b_all.at[:, 1 - core], one_ss.at[1], one_rs.at[1], twin).wait_recv()
    xb[...] = dot(b_all[...].reshape(N, N), tab_ref[FWD_X])

    arrived(LINES)
    asked = jnp.concatenate([l_all[p] for p in order], axis=0)
    resid = (rho_weight * (1.0 - eta_step * rho_weight)) * old - asked
    asked = dot_parts(resid, tab_ref[FWD_X]) * (1.0 / math.sqrt(N))
    sheared(nothing, lambda j, rows: (asked[j : j + 1, :HALF], asked[j : j + 1, HALF:]), nothing, -1)
    size = N // PARTS
    for i, rows in enumerate(parts):
        y = dot(work_b[:, rows].reshape(PEERS * size, N), tab_ref[FWD_X])
        total = jnp.zeros((size, N), F32)
        for j, p in enumerate(order):
            here = y[j * size : (j + 1) * size]
            total = total + jnp.concatenate(turned(here[:, :HALF], here[:, HALF:], tab_a, p, rows, -1), axis=1)
        s_sum[rows] = total
        s_send[rows] = total.astype(BF16)
        s_twins[i].start()

    def take_twin(i, rows):
        s_twins[i].wait_recv()
        total = s_sum[rows] + s_recv[rows].astype(F32)
        s_sum[rows] = total
        xs[rows] = xb[rows] - tau_step * total

    def send_back():
        blocks = s_sum[...].astype(BF16).reshape(PEERS, 2, ROWS, N)
        blocks = jnp.where(core == 0, blocks[:, 0], blocks[:, 1]).reshape(HALF, N)
        k_send[...] = dot(blocks, tab_ref[INV_X]).astype(BF16).reshape(PEERS, ROWS, N)
        for p in range(PEERS):
            k_copy(p, my_slot).start()

    new = projected(take_twin, send_back)
    for j, p in enumerate(order):
        new_send[j] = new[j : j + 1]
    for j, p in enumerate(order):
        new_copy(j, p, my_slot).start()

    arrived(BACK)
    for q in range(PEERS):
        vol_made[:, q, :] = b_own[q] - tau_step * k_all[q].astype(F32)
    leave_vol = pltpu.make_async_copy(vol_made, vol_out, in_sem.at[0])
    leave_phase = pltpu.make_async_copy(phase_made, phase_out, in_sem.at[1])
    leave_dual = pltpu.make_async_copy(dual_made, dual_out, in_sem.at[2])
    leave_vol.start()
    arrived(OLD)
    phase_new = base + (eta_step * rho_weight) * jnp.concatenate([old_all[q] for q in range(PEERS)], axis=0)
    phase_made[...] = phase_new
    leave_phase.start()
    arrived(NEW)
    after = jnp.concatenate([new_all[q] for q in range(PEERS)], axis=0)
    dual_made[...] = dual_ref[...] + rho_weight * (phase_new - after)
    leave_dual.start()

    for i, group in enumerate(groups):
        copy(group, group, sent.at[i], came.at[i], twin).wait_send()
    for one in [v_twin, b_twin, halo_up, halo_down] + s_twins:
        one.wait_send()
    for leave in (leave_vol, leave_phase, leave_dual):
        leave.wait()


def hand_over(phase_in, vol_in, dual_in, phase_out, vol_out, dual_out):
    phase_out[...] = phase_in[...]
    vol_out[...] = vol_in[...]
    dual_out[...] = dual_in[...]


def shards(volume, phase, dual, probe_real, probe_imag, intensity, offsets, angle_index):
    tables = jnp.asarray(packed_tables()).astype(BF16)
    in_vmem = pl.BlockSpec(memory_space=pltpu.VMEM)
    in_place = pl.BlockSpec(memory_space=pltpu.HBM)
    dma = pltpu.SemaphoreType.DMA
    vmem = pltpu.VMEM
    blocks = (PEERS, ROWS, N)
    lines = (PEERS, 1, N)
    results = (
        jax.ShapeDtypeStruct(phase.shape[1:], F32),
        jax.ShapeDtypeStruct(volume.shape, F32),
        jax.ShapeDtypeStruct(dual.shape[1:], F32),
    )
    made = pl.pallas_call(
        step_kernel,
        out_shape=results,
        in_specs=[in_place] * 9,
        out_specs=(in_place,) * 3,
        scratch_shapes=[
            pltpu.SMEM((1, SHOTS), jnp.int32),
            pltpu.SMEM((1,), jnp.int32),
            vmem(volume.shape, F32),
            vmem((8, N), F32),
            vmem((8, N), F32),
            vmem((HALF, HALF), F32),
            vmem((HALF, HALF), F32),
            vmem((SHOTS, HALF, HALF), F32),
            vmem(tables.shape, BF16),
            vmem((8, N), BF16),
            vmem((8, 128), F32),
            vmem((PEERS, 8, 128), F32),
            vmem(blocks, BF16),
            vmem((PEERS, 2, ROWS, N), BF16),
            vmem(blocks, BF16),
            vmem((PEERS, 2, ROWS, N), BF16),
            vmem(blocks, F32),
            vmem((2, ROWS, N), BF16),
            vmem((TILES, 8, N), BF16),
            vmem((TILES, 8, N), BF16),
            vmem((TILES, 8, N), BF16),
            vmem(lines, F32),
            vmem(lines, F32),
            vmem(lines, F32),
            vmem(lines, F32),
            vmem(lines, F32),
            vmem(lines, F32),
            vmem(blocks, BF16),
            vmem(blocks, BF16),
            vmem((N, N), BF16),
            vmem((N, N), BF16),
            vmem((PEERS, N, N), BF16),
            vmem((PEERS, N, N), BF16),
            vmem(volume.shape, F32),
            vmem((8, N), F32),
            vmem((8, N), F32),
            vmem((PEERS, 3, N, HALF), F32),
            vmem((PEERS, 3, HALF, N), F32),
            vmem((N, N), F32),
            vmem((N, N), F32),
            vmem((N, N), F32),
            vmem((SHOTS, 2, HALF, HALF), F32),
            dma((9,)),
            dma((9,)),
            dma((4,)),
            dma((4,)),
            dma((PARTS,)),
            dma((PARTS,)),
            dma((9,)),
        ],
        compiler_params=pltpu.CompilerParams(collective_id=0, has_side_effects=True),
    )(offsets, angle_index, volume, phase[0], dual[0], probe_real, probe_imag, intensity[0], tables)
    phase_new, volume_new, dual_new = pl.pallas_call(
        hand_over, out_shape=results, in_specs=[in_vmem] * 3, out_specs=(in_vmem,) * 3
    )(*made)
    return (phase_new[None], volume_new, dual_new[None])


def solution(mesh):
    placed = (
        P("ang", "tile", None),
        P("ang", "tile", None),
        P("ang", "tile", None),
        P(),
        P(),
        P("ang", "tile", None, None),
        P("ang", "tile"),
        P("ang"),
    )
    return jax.shard_map(
        shards,
        mesh=mesh,
        in_specs=placed,
        out_specs=(P("ang", "tile", None), P("ang", "tile", None), P("ang", "tile", None)),
        check_vma=False,
    )
```

time: 49.9 us -> 42.3 us (0.85)
  Pallas kernels: 48.5 us -> 40.9 us
    pallas_call x1, Pallas kernels: 46.9 us -> 39.3 us  [shards(): pl.pallas_call(step_kernel, out_shape=results, in_specs=[in_place] * 9, o...]
where the time goes in v2:
time: 42.3 us; the launch traced here: 42.1 us
  Pallas kernels  40.9 us (97%)
  between operations  1.29 us (3%)
    pallas_call x1, Pallas kernels, shards(): pl.pallas_call(step_kernel, out_shape=results, in_specs=[in_place] * 9, o...  39.3 us
    pallas_call x1, Pallas kernels, shards(): pl.pallas_call(hand_over, out_shape=results, in_specs=[in_vmem] * 3, out_...  1.57 us

profile of v2, /device:TPU:1, one launch (start us, length us, event | category | flops | bytes accessed | tf_op | source)
XLA Modules:
  0.0 42.1 jit_solution(4767699673446285435)
XLA Ops:
  1.3 39.3 %shard_map.112 = (f32[8,256]{1,0:T(8,128)}, f32[16,8,256]{2,1,0:T(8,128)}, f32[8,256]{1,0:T(8,128)}) custom-call(s32[1,4]{1,0:T(1,128)} %offsets_in.1, s32[1]{0:T(128)S(6)} %copy.12.angle_in, f32[16,8,256]{2,1,0:T(8,128)} %vol_in.1, f32[8,256]{1,0:T(8,128)} %bitcast.6, f32[8,256]{1,0:T(8,128)} %bitcast.7, f32[128,128]{1,0:T(8,128)} %pr_in.1, ...), custom_call_target="tpu_custom_call" | custom-call | tf_op jit(solution)/shard_map/pallas_call | solution.py:430
  40.6 1.6 %shard_map.113 = (f32[8,256]{1,0:T(8,128)}, f32[16,8,256]{2,1,0:T(8,128)}, f32[8,256]{1,0:T(8,128)}) custom-call(f32[8,256]{1,0:T(8,128)} %get-tuple-element.9.phase_in, f32[16,8,256]{2,1,0:T(8,128)} %get-tuple-element.10.vol_in, f32[8,256]{1,0:T(8,128)} %get-tuple-element.11.dual_in), custom_call_target="tpu_custom_call" | custom-call | tf_op jit(solution)/shard_map/pallas_call | solution.py:488

commit v3 on v2

--- a/solution.py
+++ b/solution.py
@@ -24,7 +24,7 @@
 STRIP = 32
 FWD_X, INV_X, FWD_Y, INV_Y = range(4)
 PHASE, GRAD, COEF, VOLUME, SMOOTH, LINES, OLD, NEW, BACK = range(9)
-PARTS = 4
+PARTS = 2
 NEAR_LAST = [4 * dy + dz for dy in (2, 1, 3, 0) for dz in range(4) if dy or dz]
 F32 = jnp.float32
 BF16 = jnp.bfloat16
@@ -196,10 +196,10 @@
     halo_up = copy(v_send.at[PEERS - 1], halo.at[0], one_ss.at[2], one_rs.at[2], (me, (tile + 1) % TILES))
     halo_down = copy(v_send.at[0], halo.at[1], one_ss.at[3], one_rs.at[3], (me, (tile + TILES - 1) % TILES))
 
+    for o in NEAR_LAST:
+        phase_copy(o, tile).start()
     for p in range(PEERS):
         coef_copy(p, mine).start()
-    for o in NEAR_LAST:
-        phase_copy(o, tile).start()
     for p in range(PEERS):
         v_copy(p, mine).start()
     halo_up.start()
@@ -286,9 +286,6 @@
 
     arrived(VOLUME)
     v_twin.start()
-    copy(v_all.at[:, 1 - core], v_all.at[:, 1 - core], one_ss.at[0], one_rs.at[0], twin).wait_recv()
-    xs[...] = dot(v_all[...].reshape(N, N), tab_ref[FWD_X])
-
     def turned(p_part, q_part, table, p, rows, sign):
         cos, sin, end = table[p, 0, rows], table[p, 1, rows], table[p, 2, rows]
         if sign > 0:
@@ -318,14 +315,15 @@
         for j in range(PEERS):
             work_b[j] = dot(tab_ref[INV_Y], work_a[j]).astype(BF16)
 
-    def projected(prepare, middle):
+    def projected(prepare, middle, groups, finish):
         sheared(prepare, lambda j, rows: (xs[rows, :HALF], xs[rows, HALF:]), middle, 1)
-        spectra = []
-        for j, p in enumerate(order):
-            y = dot(work_b[j], tab_ref[FWD_X])
-            turn = turned(y[:, :HALF], y[:, HALF:], tab_a, p, whole, 1)
-            spectra.append(jnp.sum(jnp.concatenate(turn, axis=1), axis=0, keepdims=True))
-        return dot_parts(jnp.concatenate(spectra, axis=0), tab_ref[INV_X]) * (1.0 / math.sqrt(N))
+        for js in groups:
+            spectra = []
+            for j in js:
+                y = dot(work_b[j], tab_ref[FWD_X])
+                turn = turned(y[:, :HALF], y[:, HALF:], tab_a, order[j], whole, 1)
+                spectra.append(jnp.sum(jnp.concatenate(turn, axis=1), axis=0, keepdims=True))
+            finish(js, dot_parts(jnp.concatenate(spectra, axis=0), tab_ref[INV_X]) * (1.0 / math.sqrt(N)))
 
     def nothing(*unused):
         pass
@@ -339,13 +337,22 @@
     for p in range(PEERS):
         l_copy(p, mine).start()
 
+    copy(v_all.at[:, 1 - core], v_all.at[:, 1 - core], one_ss.at[0], one_rs.at[0], twin).wait_recv()
+    xs[...] = dot(v_all[...].reshape(N, N), tab_ref[FWD_X])
+
     arrived(SMOOTH)
     b_twin.start()
-    old = projected(nothing, nothing)
-    for j, p in enumerate(order):
-        old_send[j] = old[j : j + 1]
-    for j, p in enumerate(order):
-        old_copy(j, p, my_slot).start()
+    kept = []
+
+    def send_old(js, lines):
+        kept.append(lines)
+        for j in js:
+            old_send[j] = lines[j : j + 1]
+        for j in js:
+            old_copy(j, order[j], my_slot).start()
+
+    projected(nothing, nothing, [range(PEERS)], send_old)
+    old = kept[0]
     copy(b_all.at[:, 1 - core], b_all.at[:, 1 - core], one_ss.at[1], one_rs.at[1], twin).wait_recv()
     xb[...] = dot(b_all[...].reshape(N, N), tab_ref[FWD_X])
 
@@ -354,13 +361,14 @@
     resid = (rho_weight * (1.0 - eta_step * rho_weight)) * old - asked
     asked = dot_parts(resid, tab_ref[FWD_X]) * (1.0 / math.sqrt(N))
     sheared(nothing, lambda j, rows: (asked[j : j + 1, :HALF], asked[j : j + 1, HALF:]), nothing, -1)
-    size = N // PARTS
+    for j, p in enumerate(order[:-1]):
+        y = dot(work_b[j], tab_ref[FWD_X])
+        turn = jnp.concatenate(turned(y[:, :HALF], y[:, HALF:], tab_a, p, whole, -1), axis=1)
+        s_sum[...] = turn if j == 0 else s_sum[...] + turn
     for i, rows in enumerate(parts):
-        y = dot(work_b[:, rows].reshape(PEERS * size, N), tab_ref[FWD_X])
-        total = jnp.zeros((size, N), F32)
-        for j, p in enumerate(order):
-            here = y[j * size : (j + 1) * size]
-            total = total + jnp.concatenate(turned(here[:, :HALF], here[:, HALF:], tab_a, p, rows, -1), axis=1)
+        y = dot(work_b[PEERS - 1, rows], tab_ref[FWD_X])
+        turn = turned(y[:, :HALF], y[:, HALF:], tab_a, order[-1], rows, -1)
+        total = s_sum[rows] + jnp.concatenate(turn, axis=1)
         s_sum[rows] = total
         s_send[rows] = total.astype(BF16)
         s_twins[i].start()
@@ -378,34 +386,28 @@
         for p in range(PEERS):
             k_copy(p, my_slot).start()
 
-    new = projected(take_twin, send_back)
-    for j, p in enumerate(order):
-        new_send[j] = new[j : j + 1]
-    for j, p in enumerate(order):
-        new_copy(j, p, my_slot).start()
+    def send_new(js, lines):
+        for j in js:
+            new_send[j] = lines[j - js[0] : j - js[0] + 1]
+        for j in js:
+            new_copy(j, order[j], my_slot).start()
+
+    projected(take_twin, send_back, [range(2), range(2, PEERS)], send_new)
 
     arrived(BACK)
     for q in range(PEERS):
-        vol_made[:, q, :] = b_own[q] - tau_step * k_all[q].astype(F32)
-    leave_vol = pltpu.make_async_copy(vol_made, vol_out, in_sem.at[0])
-    leave_phase = pltpu.make_async_copy(phase_made, phase_out, in_sem.at[1])
-    leave_dual = pltpu.make_async_copy(dual_made, dual_out, in_sem.at[2])
-    leave_vol.start()
+        vol_out[:, q, :] = b_own[q] - tau_step * k_all[q].astype(F32)
     arrived(OLD)
     phase_new = base + (eta_step * rho_weight) * jnp.concatenate([old_all[q] for q in range(PEERS)], axis=0)
-    phase_made[...] = phase_new
-    leave_phase.start()
+    phase_out[...] = phase_new
     arrived(NEW)
     after = jnp.concatenate([new_all[q] for q in range(PEERS)], axis=0)
-    dual_made[...] = dual_ref[...] + rho_weight * (phase_new - after)
-    leave_dual.start()
+    dual_out[...] = dual_ref[...] + rho_weight * (phase_new - after)
 
     for i, group in enumerate(groups):
         copy(group, group, sent.at[i], came.at[i], twin).wait_send()
     for one in [v_twin, b_twin, halo_up, halo_down] + s_twins:
         one.wait_send()
-    for leave in (leave_vol, leave_phase, leave_dual):
-        leave.wait()
 
 
 def hand_over(phase_in, vol_in, dual_in, phase_out, vol_out, dual_out):
@@ -431,7 +433,7 @@
         step_kernel,
         out_shape=results,
         in_specs=[in_place] * 9,
-        out_specs=(in_place,) * 3,
+        out_specs=(in_vmem,) * 3,
         scratch_shapes=[
             pltpu.SMEM((1, SHOTS), jnp.int32),
             pltpu.SMEM((1,), jnp.int32),
@@ -483,10 +485,10 @@
             dma((PARTS,)),
             dma((9,)),
         ],
-        compiler_params=pltpu.CompilerParams(collective_id=0, has_side_effects=True),
-    )(offsets, angle_index, volume, phase[0], dual[0], probe_real, probe_imag, intensity[0], tables)
+        compiler_params=pltpu.CompilerParams(collective_id=0, has_side_effects=True, vmem_limit_bytes=24 << 20),
+    )(*[pltpu.with_memory_space_constraint(x, pltpu.HBM) for x in (offsets,)], angle_index, *[pltpu.with_memory_space_constraint(x, pltpu.HBM) for x in (volume, phase[0], dual[0], probe_real, probe_imag, intensity[0], tables)])
     phase_new, volume_new, dual_new = pl.pallas_call(
-        hand_over, out_shape=results, in_specs=[in_vmem] * 3, out_specs=(in_vmem,) * 3
+        hand_over, out_shape=results, in_specs=[in_vmem] * 3, out_specs=(in_vmem,) * 3, compiler_params=pltpu.CompilerParams(vmem_limit_bytes=4 << 20)
     )(*made)
     return (phase_new[None], volume_new, dual_new[None])
 

time: 42.3 us -> 40 us (0.946)
  Pallas kernels: 40.9 us -> 38.6 us
    pallas_call x1, Pallas kernels: 39.3 us -> 37.9 us  [shards(): pl.pallas_call(step_kernel, out_shape=results, in_specs=[in_place] * 9, o...]
    pallas_call x1, Pallas kernels: 1.57 us -> 0.67 us  [shards(): pl.pallas_call(hand_over, out_shape=results, in_specs=[in_vmem] * 3, out_...]
where the time goes in v3:
time: 40 us; the launch traced here: 39.9 us
  Pallas kernels  38.6 us (96%)
  between operations  1.29 us (3%)
    pallas_call x1, Pallas kernels, shards(): pl.pallas_call(step_kernel, out_shape=results, in_specs=[in_place] * 9, o...  37.9 us

profile of v3, /device:TPU:1, one launch (start us, length us, event | category | flops | bytes accessed | tf_op | source)
XLA Modules:
  0.0 39.9 jit_solution(15713735059176980644)
XLA Ops:
  1.3 37.9 %shard_map.112 = (f32[8,256]{1,0:T(8,128)S(1)}, f32[16,8,256]{2,1,0:T(8,128)S(1)}, f32[8,256]{1,0:T(8,128)S(1)}) custom-call(s32[1,4]{1,0:T(1,128)} %offsets_in.1, s32[1]{0:T(128)S(6)} %copy.12.angle_in, f32[16,8,256]{2,1,0:T(8,128)} %vol_in.1, f32[8,256]{1,0:T(8,128)} %bitcast.6, f32[8,256]{1,0:T(8,128)} %bitcast.7, f32[128,128]{1,0:T(8,128)} %pr_in.1, ...), custom_call_target="tpu_custom_call" | custom-call | tf_op jit(solution)/shard_map/pallas_call | solution.py:432
  39.2 0.7 %shard_map.113 = (f32[8,256]{1,0:T(8,128)}, f32[16,8,256]{2,1,0:T(8,128)}, f32[8,256]{1,0:T(8,128)}) custom-call(f32[8,256]{1,0:T(8,128)S(1)} %get-tuple-element.9.phase_in, f32[16,8,256]{2,1,0:T(8,128)S(1)} %get-tuple-element.10.vol_in, f32[8,256]{1,0:T(8,128)S(1)} %get-tuple-element.11.dual_in), custom_call_target="tpu_custom_call" | custom-call | tf_op jit(solution)/shard_map/pallas_call | solution.py:490

commit v4 on v3

--- a/solution.py
+++ b/solution.py
@@ -25,6 +25,9 @@
 FWD_X, INV_X, FWD_Y, INV_Y = range(4)
 PHASE, GRAD, COEF, VOLUME, SMOOTH, LINES, OLD, NEW, BACK = range(9)
 PARTS = 2
+AWAY = [2, 2, 1, 1, 1, 1, 0, 0]
+MOVED = (0, 1, 4, 5)
+LATE = 4
 NEAR_LAST = [4 * dy + dz for dy in (2, 1, 3, 0) for dz in range(4) if dy or dz]
 F32 = jnp.float32
 BF16 = jnp.bfloat16
@@ -87,10 +90,10 @@
     offsets_in, angle_in, vol_in, phase_in, dual_in, pr_in, pi_in, inten_in, tab_in,
     phase_out, vol_out, dual_out,
     offsets_ref, angle_ref, vol_ref, phase_ref, dual_ref, pr_ref, pi_ref, inten_ref, tab_ref, phase_send,
-    coef_send, coef_all, v_send, v_all, b_send, b_all, b_own, halo, phase_all, g_send, g_all, l_send, l_all,
+    coef_send, coef_all, coef_other, v_send, v_all, b_send, b_all, b_own, halo, phase_all, g_send, g_all, l_send, l_all,
     old_send, old_all, new_send, new_all, k_send, k_all, s_send, s_recv,
     work_a, work_b, vol_made, phase_made, dual_made, tab_a, tab_b, xs, xb, s_sum, wave,
-    sent, came, one_ss, one_rs, part_ss, part_rs, in_sem,
+    sent, came, near_rs, one_ss, one_rs, part_ss, part_rs, in_sem,
 ):
     me = lax.axis_index("ang")
     tile = lax.axis_index("tile")
@@ -120,6 +123,8 @@
         pl.semaphore_signal(barrier, inc=1, device_id=beside(o), device_id_type=MESH)
     for p in range(PEERS):
         pl.semaphore_signal(barrier, inc=1, device_id=peer(p), device_id_type=MESH)
+    for p in range(PEERS):
+        pl.semaphore_signal(barrier, inc=1, device_id=(2 * p + 1 - core, far_tile), device_id_type=MESH)
     pl.semaphore_signal(barrier, inc=1, device_id=twin, device_id_type=MESH)
 
     loads = [
@@ -147,7 +152,7 @@
     for q in range(PEERS):
         v_send[q] = vol_ref[:, q, :].astype(BF16)
 
-    pl.semaphore_wait(barrier, TILES + PEERS)
+    pl.semaphore_wait(barrier, TILES + 2 * PEERS)
 
     def copy(src, dst, send, recv, device):
         return pltpu.make_async_remote_copy(
@@ -169,8 +174,11 @@
     def g_copy(o, slot):
         return copy(g_send.at[beside(o)[1]], g_all.at[slot], sent.at[1], came.at[1], beside(o))
 
-    def l_copy(p, slot):
-        return copy(l_send.at[slot_of(p)], l_all.at[slot], sent.at[5], came.at[5], peer(p))
+    def l_copy(j, p, slot):
+        if j in MOVED:
+            row, came_at = slot + PEERS * (1 - core), jnp.where(core == 1, AWAY[j], 3)
+            return copy(l_send.at[slot_of(p)], l_all.at[row], sent.at[5], near_rs.at[came_at], (2 * p + 1, far_tile))
+        return copy(l_send.at[slot_of(p)], l_all.at[slot], sent.at[5], near_rs.at[AWAY[j]], peer(p))
 
     def old_copy(j, p, slot):
         return copy(old_send.at[j], old_all.at[slot], sent.at[6], came.at[6], peer(p))
@@ -182,7 +190,7 @@
         return copy(k_send.at[p], k_all.at[slot], sent.at[8], came.at[8], peer(p))
 
     others = pl.ds(0, TILES - 1)
-    groups = [phase_all.at[others], g_all.at[others], coef_all, v_send, b_send, l_send, old_send, new_send, k_send]
+    groups = [phase_all.at[others], g_all.at[others], coef_all, v_send, b_send, l_send, old_all, new_send, k_send]
 
     def arrived(group):
         copy(groups[group], groups[group], sent.at[group], came.at[group], twin).wait_recv()
@@ -193,6 +201,8 @@
     s_twins = [
         copy(s_send.at[rows], s_recv.at[rows], part_ss.at[i], part_rs.at[i], twin) for i, rows in enumerate(parts)
     ]
+    coef_twin = copy(coef_all, coef_other, one_ss.at[4], one_rs.at[4], twin)
+    old_twin = copy(old_send.at[pl.ds(0, PEERS)], old_send.at[pl.ds(PEERS, PEERS)], one_ss.at[5], one_rs.at[5], twin)
     halo_up = copy(v_send.at[PEERS - 1], halo.at[0], one_ss.at[2], one_rs.at[2], (me, (tile + 1) % TILES))
     halo_down = copy(v_send.at[0], halo.at[1], one_ss.at[3], one_rs.at[3], (me, (tile + TILES - 1) % TILES))
 
@@ -257,35 +267,48 @@
     for p in range(PEERS):
         b_copy(p, mine).start()
 
-    arrived(COEF)
-
-    lane = lax.broadcasted_iota(jnp.int32, (N, HALF), 1)
-    line = lax.broadcasted_iota(jnp.int32, (N, HALF), 0)
-    freq_a = jnp.where(lane == 0, HALF, lane).astype(F32) * (1.0 / N)
-    row_a = (line - HALF).astype(F32)
-    lane_b = lax.broadcasted_iota(jnp.int32, (HALF, N), 1)
-    line_b = lax.broadcasted_iota(jnp.int32, (HALF, N), 0)
-    freq_b = jnp.where(line_b == 0, HALF, line_b).astype(F32) * (1.0 / N)
-    row_b = (lane_b - HALF).astype(F32)
-
-    def angle_tables(p, carry):
-        coef = coef_all[p]
-        shift = coef[0:1, :]
-        sin, cos = sincos_turns((row_a * shift) * freq_a)
-        tab_a[p, 0] = jnp.where(lane == 0, 1.0, cos)
-        tab_a[p, 1] = jnp.where(lane == 0, 0.0, sin)
-        tab_a[p, 2] = cos
-        shift = jnp.concatenate([coef[4:5, :], coef[4:5, :]], axis=1)
-        sin, cos = sincos_turns((row_b * shift) * freq_b)
-        tab_b[p, 0] = jnp.where(line_b == 0, 1.0, cos)
-        tab_b[p, 1] = jnp.where(line_b == 0, 0.0, sin)
-        tab_b[p, 2] = cos
-        return carry
-
-    lax.fori_loop(0, PEERS, angle_tables, 0)
-
     arrived(VOLUME)
     v_twin.start()
+    arrived(COEF)
+    coef_twin.start()
+
+    def counted(rows, columns, dim):
+        return lax.broadcasted_iota(jnp.int32, (rows, columns), dim)
+
+    first_lane = counted(8, HALF, 1) == 0
+    first_line = counted(8, N, 0) == 0
+    lanes = counted(1, HALF, 1)
+    freq_a = jnp.where(lanes == 0, HALF, lanes).astype(F32) * (1.0 / N)
+    column_b = (counted(1, N, 1) - HALF).astype(F32) * (1.0 / N)
+
+    def angle_tables(coefs, source, p):
+        coef = coefs[source]
+        step = coef[0:1, :] * freq_a
+        sin_i, cos_i = sincos_turns(counted(8, HALF, 0).astype(F32) * step)
+        sin_j, cos_j = sincos_turns((8 * counted(32, HALF, 0) - HALF).astype(F32) * step)
+        for j in range(32):
+            rows = slice(8 * j, 8 * j + 8)
+            cos = cos_i * cos_j[j : j + 1] - sin_i * sin_j[j : j + 1]
+            sin = sin_i * cos_j[j : j + 1] + cos_i * sin_j[j : j + 1]
+            tab_a[p, 0, rows] = jnp.where(first_lane, 1.0, cos)
+            tab_a[p, 1, rows] = jnp.where(first_lane, 0.0, sin)
+            tab_a[p, 2, rows] = cos
+        step = jnp.concatenate([coef[4:5, :], coef[4:5, :]], axis=1) * column_b
+        sin_i, cos_i = sincos_turns(counted(8, N, 0).astype(F32) * step)
+        sin_j, cos_j = sincos_turns((8 * counted(16, N, 0)).astype(F32) * step)
+        unused, cos_end = sincos_turns(HALF * step)
+        for j in range(16):
+            rows = slice(8 * j, 8 * j + 8)
+            cos = cos_i * cos_j[j : j + 1] - sin_i * sin_j[j : j + 1]
+            sin = sin_i * cos_j[j : j + 1] + cos_i * sin_j[j : j + 1]
+            tab_b[p, 0, rows] = cos
+            tab_b[p, 1, rows] = sin
+            tab_b[p, 2, rows] = jnp.where(first_line, cos_end, cos) if j == 0 else cos
+
+    pl.loop(0, PEERS)(lambda p: angle_tables(coef_all, p, p))
+    coef_twin.wait_recv()
+    pl.loop(0, LATE)(lambda j: angle_tables(coef_other, 2 * ((x_me + 2 - j // 2) % 4) + j % 2, PEERS + j))
+
     def turned(p_part, q_part, table, p, rows, sign):
         cos, sin, end = table[p, 0, rows], table[p, 1, rows], table[p, 2, rows]
         if sign > 0:
@@ -294,84 +317,115 @@
 
     whole = slice(None)
 
-    def sheared(prepare, start, middle, sign):
+    def sheared(place, js, prepare, start, middle, sign):
         for i, part in enumerate(parts):
             prepare(i, part)
-            for j, p in enumerate(order):
+            for j in js:
                 for r in range(part.start, part.stop, STRIP):
                     rows = slice(r, r + STRIP)
                     first, second = start(j, rows)
-                    first, second = turned(first, second, tab_a, p, rows, sign)
+                    first, second = turned(first, second, tab_a, place[j], rows, sign)
                     work_a[j, rows, :HALF] = first.astype(BF16)
                     work_a[j, rows, HALF:] = second.astype(BF16)
         middle()
-        for j in range(PEERS):
+        for j in js:
             work_b[j] = dot(work_a[j], tab_ref[INV_X]).astype(BF16)
-        for j, p in enumerate(order):
+        for j in js:
             y = dot(tab_ref[FWD_Y], work_b[j])
-            first, second = turned(y[:HALF], y[HALF:], tab_b, p, whole, sign)
+            first, second = turned(y[:HALF], y[HALF:], tab_b, place[j], whole, sign)
             work_a[j, :HALF] = first.astype(BF16)
             work_a[j, HALF:] = second.astype(BF16)
-        for j in range(PEERS):
+        for j in js:
             work_b[j] = dot(tab_ref[INV_Y], work_a[j]).astype(BF16)
 
     def projected(prepare, middle, groups, finish):
-        sheared(prepare, lambda j, rows: (xs[rows, :HALF], xs[rows, HALF:]), middle, 1)
+        sheared(order, range(PEERS), prepare, lambda j, rows: (xs[rows, :HALF], xs[rows, HALF:]), middle, 1)
         for js in groups:
             spectra = []
             for j in js:
                 y = dot(work_b[j], tab_ref[FWD_X])
                 turn = turned(y[:, :HALF], y[:, HALF:], tab_a, order[j], whole, 1)
                 spectra.append(jnp.sum(jnp.concatenate(turn, axis=1), axis=0, keepdims=True))
-            finish(js, dot_parts(jnp.concatenate(spectra, axis=0), tab_ref[INV_X]) * (1.0 / math.sqrt(N)))
+            finish(js, spectra)
+
+    def lines_of(spectra):
+        return dot_parts(jnp.concatenate(spectra, axis=0), tab_ref[INV_X]) * (1.0 / math.sqrt(N))
 
     def nothing(*unused):
         pass
+
+    copy(v_all.at[:, 1 - core], v_all.at[:, 1 - core], one_ss.at[0], one_rs.at[0], twin).wait_recv()
+    xs[...] = dot(v_all[...].reshape(N, N), tab_ref[FWD_X])
 
     arrived(GRAD)
     grad = jnp.sum(g_all[...].astype(F32), axis=0)
     base = phase_ref[...] - eta_step * (grad + dual_ref[...] + rho_weight * phase_ref[...])
-    lines = rho_weight * base + dual_ref[...]
+    lines = dot_parts(rho_weight * base + dual_ref[...], tab_ref[FWD_X])
     for q in range(PEERS):
         l_send[q] = lines[q : q + 1]
-    for p in range(PEERS):
-        l_copy(p, mine).start()
-
-    copy(v_all.at[:, 1 - core], v_all.at[:, 1 - core], one_ss.at[0], one_rs.at[0], twin).wait_recv()
-    xs[...] = dot(v_all[...].reshape(N, N), tab_ref[FWD_X])
+    for j, p in enumerate(order):
+        l_copy(j, p, mine).start()
+
+    def send_old(js, spectra):
+        for j in js:
+            old_send[j] = spectra[j - js[0]]
+        for j in js:
+            old_copy(j, order[j], my_slot).start()
+
+    projected(nothing, nothing, [range(PEERS)], send_old)
+    old_twin.start()
 
     arrived(SMOOTH)
     b_twin.start()
-    kept = []
-
-    def send_old(js, lines):
-        kept.append(lines)
-        for j in js:
-            old_send[j] = lines[j : j + 1]
-        for j in js:
-            old_copy(j, order[j], my_slot).start()
-
-    projected(nothing, nothing, [range(PEERS)], send_old)
-    old = kept[0]
-    copy(b_all.at[:, 1 - core], b_all.at[:, 1 - core], one_ss.at[1], one_rs.at[1], twin).wait_recv()
-    xb[...] = dot(b_all[...].reshape(N, N), tab_ref[FWD_X])
-
-    arrived(LINES)
-    asked = jnp.concatenate([l_all[p] for p in order], axis=0)
-    resid = (rho_weight * (1.0 - eta_step * rho_weight)) * old - asked
-    asked = dot_parts(resid, tab_ref[FWD_X]) * (1.0 / math.sqrt(N))
-    sheared(nothing, lambda j, rows: (asked[j : j + 1, :HALF], asked[j : j + 1, HALF:]), nothing, -1)
-    for j, p in enumerate(order[:-1]):
-        y = dot(work_b[j], tab_ref[FWD_X])
-        turn = jnp.concatenate(turned(y[:, :HALF], y[:, HALF:], tab_a, p, whole, -1), axis=1)
-        s_sum[...] = turn if j == 0 else s_sum[...] + turn
+
+    def lines_in(group, rows):
+        here = l_all.at[pl.ds(0, rows)]
+        copy(here, here, sent.at[5], near_rs.at[group], twin).wait_recv()
+
+    def backproject(place, js, asked, added):
+        sheared(place, js, nothing, lambda j, rows: (asked[j][:, :HALF], asked[j][:, HALF:]), nothing, -1)
+        for j in added:
+            y = dot(work_b[j], tab_ref[FWD_X])
+            turn = turned(y[:, :HALF], y[:, HALF:], tab_a, place[j], whole, -1)
+            s_sum[...] += jnp.concatenate(turn, axis=1)
+
+    def spectrum_asked(row_old, row_line):
+        mine_part = (rho_weight * (1.0 - eta_step * rho_weight) / N) * old_send[row_old]
+        return mine_part - (1.0 / math.sqrt(N)) * l_all[row_line]
+
+    s_sum[...] = jnp.zeros((N, N), F32)
+
+    @pl.when(core == 1)
+    def _():
+        for group, js in enumerate([(6, 7), (2, 3, 4, 5), (0, 1)]):
+            lines_in(group, len(js))
+            backproject(order, js, {j: spectrum_asked(j, order[j]) for j in js}, js)
+        lines_in(3, LATE)
+
+    @pl.when(core == 0)
+    def _():
+        lines_in(0, 2)
+        lines_in(1, 2)
+
+    old_twin.wait_recv()
+    late = range(LATE)
+    place = [jnp.where(core == 1, PEERS + j, order[LATE + j]) for j in late]
+    asked = [
+        spectrum_asked(LATE + j + core * (PEERS - LATE), jnp.where(core == 1, PEERS + order[j], order[LATE + j]))
+        for j in late
+    ]
+    backproject(place, late, asked, late[:-1])
+    last = LATE - 1
     for i, rows in enumerate(parts):
-        y = dot(work_b[PEERS - 1, rows], tab_ref[FWD_X])
-        turn = turned(y[:, :HALF], y[:, HALF:], tab_a, order[-1], rows, -1)
+        y = dot(work_b[last, rows], tab_ref[FWD_X])
+        turn = turned(y[:, :HALF], y[:, HALF:], tab_a, place[last], rows, -1)
         total = s_sum[rows] + jnp.concatenate(turn, axis=1)
         s_sum[rows] = total
         s_send[rows] = total.astype(BF16)
         s_twins[i].start()
+
+    copy(b_all.at[:, 1 - core], b_all.at[:, 1 - core], one_ss.at[1], one_rs.at[1], twin).wait_recv()
+    xb[...] = dot(b_all[...].reshape(N, N), tab_ref[FWD_X])
 
     def take_twin(i, rows):
         s_twins[i].wait_recv()
@@ -386,27 +440,27 @@
         for p in range(PEERS):
             k_copy(p, my_slot).start()
 
-    def send_new(js, lines):
-        for j in js:
-            new_send[j] = lines[j - js[0] : j - js[0] + 1]
+    def send_new(js, spectra):
+        for j in js:
+            new_send[j] = spectra[j - js[0]]
         for j in js:
             new_copy(j, order[j], my_slot).start()
 
-    projected(take_twin, send_back, [range(2), range(2, PEERS)], send_new)
+    projected(take_twin, send_back, [range(2), range(2, 6), range(6, PEERS)], send_new)
 
     arrived(BACK)
     for q in range(PEERS):
         vol_out[:, q, :] = b_own[q] - tau_step * k_all[q].astype(F32)
     arrived(OLD)
-    phase_new = base + (eta_step * rho_weight) * jnp.concatenate([old_all[q] for q in range(PEERS)], axis=0)
+    phase_new = base + (eta_step * rho_weight) * lines_of([old_all[q] for q in range(PEERS)])
     phase_out[...] = phase_new
     arrived(NEW)
-    after = jnp.concatenate([new_all[q] for q in range(PEERS)], axis=0)
+    after = lines_of([new_all[q] for q in range(PEERS)])
     dual_out[...] = dual_ref[...] + rho_weight * (phase_new - after)
 
     for i, group in enumerate(groups):
         copy(group, group, sent.at[i], came.at[i], twin).wait_send()
-    for one in [v_twin, b_twin, halo_up, halo_down] + s_twins:
+    for one in [v_twin, b_twin, coef_twin, old_twin, halo_up, halo_down] + s_twins:
         one.wait_send()
 
 
@@ -447,6 +501,7 @@
             vmem((8, N), BF16),
             vmem((8, 128), F32),
             vmem((PEERS, 8, 128), F32),
+            vmem((PEERS, 8, 128), F32),
             vmem(blocks, BF16),
             vmem((PEERS, 2, ROWS, N), BF16),
             vmem(blocks, BF16),
@@ -457,8 +512,8 @@
             vmem((TILES, 8, N), BF16),
             vmem((TILES, 8, N), BF16),
             vmem(lines, F32),
-            vmem(lines, F32),
-            vmem(lines, F32),
+            vmem((2 * PEERS, 1, N), F32),
+            vmem((2 * PEERS, 1, N), F32),
             vmem(lines, F32),
             vmem(lines, F32),
             vmem(lines, F32),
@@ -471,8 +526,8 @@
             vmem(volume.shape, F32),
             vmem((8, N), F32),
             vmem((8, N), F32),
-            vmem((PEERS, 3, N, HALF), F32),
-            vmem((PEERS, 3, HALF, N), F32),
+            vmem((PEERS + LATE, 3, N, HALF), F32),
+            vmem((PEERS + LATE, 3, HALF, N), F32),
             vmem((N, N), F32),
             vmem((N, N), F32),
             vmem((N, N), F32),
@@ -480,7 +535,8 @@
             dma((9,)),
             dma((9,)),
             dma((4,)),
-            dma((4,)),
+            dma((6,)),
+            dma((6,)),
             dma((PARTS,)),
             dma((PARTS,)),
             dma((9,)),

time: 40 us -> 38.6 us (0.965)
  Pallas kernels: 38.6 us -> 37.1 us
    pallas_call x1, Pallas kernels: 37.9 us -> 36.5 us  [shards(): pl.pallas_call(step_kernel, out_shape=results, in_specs=[in_place] * 9, o...]
where the time goes in v4:
time: 38.6 us; the launch traced here: 38.4 us
  Pallas kernels  37.1 us (96%)
  between operations  1.29 us (3%)
    pallas_call x1, Pallas kernels, shards(): pl.pallas_call(step_kernel, out_shape=results, in_specs=[in_place] * 9, o...  36.5 us

profile of v4, /device:TPU:1, one launch (start us, length us, event | category | flops | bytes accessed | tf_op | source)
XLA Modules:
  0.0 38.4 jit_solution(9005773852030956167)
XLA Ops:
  1.3 36.5 %shard_map.112 = (f32[8,256]{1,0:T(8,128)S(1)}, f32[16,8,256]{2,1,0:T(8,128)S(1)}, f32[8,256]{1,0:T(8,128)S(1)}) custom-call(s32[1,4]{1,0:T(1,128)} %offsets_in.1, s32[1]{0:T(128)S(6)} %copy.12.angle_in, f32[16,8,256]{2,1,0:T(8,128)} %vol_in.1, f32[8,256]{1,0:T(8,128)} %bitcast.6, f32[8,256]{1,0:T(8,128)} %bitcast.7, f32[128,128]{1,0:T(8,128)} %pr_in.1, ...), custom_call_target="tpu_custom_call" | custom-call | tf_op jit(solution)/shard_map/pallas_call | solution.py:486
  37.8 0.7 %shard_map.113 = (f32[8,256]{1,0:T(8,128)}, f32[16,8,256]{2,1,0:T(8,128)}, f32[8,256]{1,0:T(8,128)}) custom-call(f32[8,256]{1,0:T(8,128)S(1)} %get-tuple-element.9.phase_in, f32[16,8,256]{2,1,0:T(8,128)S(1)} %get-tuple-element.10.vol_in, f32[8,256]{1,0:T(8,128)S(1)} %get-tuple-element.11.dual_in), custom_call_target="tpu_custom_call" | custom-call | tf_op jit(solution)/shard_map/pallas_call | solution.py:546

commit v5 on v4

--- a/solution.py
+++ b/solution.py
@@ -222,10 +222,13 @@
     arrived(PHASE)
 
     sin, cos = sincos_turns(phase_all[...].astype(F32).reshape(BAND_ROWS, N))
+    column = lax.broadcasted_iota(jnp.int32, (BAND_ROWS, HALF), 1)
     waves = []
     for s in range(SHOTS):
-        back = (N - offsets_ref[0, s]) % N
-        c, n = pltpu.roll(cos, back, 1)[:, :HALF], pltpu.roll(sin, back, 1)[:, :HALF]
+        back = (N - offsets_ref[0, s]) % HALF
+        from_left = column >= offsets_ref[0, s]
+        c = pltpu.roll(jnp.where(from_left, cos[:, :HALF], cos[:, HALF:]), back, 1)
+        n = pltpu.roll(jnp.where(from_left, sin[:, :HALF], sin[:, HALF:]), back, 1)
         wave_r = pr_ref[...] * c - pi_ref[...] * n
         wave_i = pr_ref[...] * n + pi_ref[...] * c
         wave[s, 0] = wave_r
@@ -247,8 +250,9 @@
     for s in range(SHOTS):
         e = leave[s * HALF : (s + 1) * HALF]
         term = 2.0 * (e[:, HALF:] * wave[s, 0] - e[:, :HALF] * wave[s, 1])
-        wide = jnp.concatenate([term, jnp.zeros((BAND_ROWS, N - HALF), F32)], axis=1)
-        image = image + pltpu.roll(wide, offsets_ref[0, s], 1)
+        term = pltpu.roll(term, offsets_ref[0, s] % HALF, 1)
+        in_left = column >= offsets_ref[0, s]
+        image = image + jnp.concatenate([jnp.where(in_left, term, 0.0), jnp.where(in_left, 0.0, term)], axis=1)
     g_send[...] = image.reshape(TILES, 8, N).astype(BF16)
     for o in NEAR_LAST:
         g_copy(o, tile).start()

time: 38.6 us -> 38.7 us (level)
  no operation moved by 1% of the time
where the time goes in v5:
time: 38.7 us; the launch traced here: 38.5 us
  Pallas kernels  37.2 us (96%)
  between operations  1.29 us (3%)
    pallas_call x1, Pallas kernels, shards(): pl.pallas_call(step_kernel, out_shape=results, in_specs=[in_place] * 9, o...  36.6 us

profile of v5, /device:TPU:1, one launch (start us, length us, event | category | flops | bytes accessed | tf_op | source)
XLA Modules:
  0.0 38.5 jit_solution(13382498495336351846)
XLA Ops:
  1.3 36.6 %shard_map.112 = (f32[8,256]{1,0:T(8,128)S(1)}, f32[16,8,256]{2,1,0:T(8,128)S(1)}, f32[8,256]{1,0:T(8,128)S(1)}) custom-call(s32[1,4]{1,0:T(1,128)} %offsets_in.1, s32[1]{0:T(128)S(6)} %copy.12.angle_in, f32[16,8,256]{2,1,0:T(8,128)} %vol_in.1, f32[8,256]{1,0:T(8,128)} %bitcast.6, f32[8,256]{1,0:T(8,128)} %bitcast.7, f32[128,128]{1,0:T(8,128)} %pr_in.1, ...), custom_call_target="tpu_custom_call" | custom-call | tf_op jit(solution)/shard_map/pallas_call | solution.py:490
  37.9 0.7 %shard_map.113 = (f32[8,256]{1,0:T(8,128)}, f32[16,8,256]{2,1,0:T(8,128)}, f32[8,256]{1,0:T(8,128)}) custom-call(f32[8,256]{1,0:T(8,128)S(1)} %get-tuple-element.9.phase_in, f32[16,8,256]{2,1,0:T(8,128)S(1)} %get-tuple-element.10.vol_in, f32[8,256]{1,0:T(8,128)S(1)} %get-tuple-element.11.dual_in), custom_call_target="tpu_custom_call" | custom-call | tf_op jit(solution)/shard_map/pallas_call | solution.py:550
